TPU v7x, 32 devices: a whole 2x2x4 slice. The times are simulated.
32 devices in a mesh: groups: 2 (over y), rows: 16 (over z, x, core).
Axes of the slice: x: 2, y: 2, z: 4, core: 2. Of those that a mesh axis runs over, the one named last changes fastest.
Arguments:
- pair_repr: bfloat16 [256, 128, 128], P('groups', 'rows'), parts along dimension 0, may hold values from -6 to 6
- single_repr: bfloat16 [256, 384], P(('groups', 'rows')), parts along dimension 0, may hold values from -6 to 6
- residue_index: int32 [256], P('groups'), parts along dimension 0, may hold values from 0 to 47
- chain_index: int32 [256], P('groups'), parts along dimension 0, may hold values from 0 to 3
- complex_index: int32 [256], P('groups'), parts along dimension 0, may hold values from 0 to 7, never falling along the last dimension, each value on 1 to 96 neighbouring positions
- pad_mask: int32 [256], P('groups'), parts along dimension 0, may hold values 0 or 1
- w_query: bfloat16 [384, 384], replicated, may hold values from -3 to 3
- w_key: bfloat16 [384, 384], replicated, may hold values from -3.1 to 3.1
- w_value: bfloat16 [384, 384], replicated, may hold values from -0.3125 to 0.3125
- w_gate: bfloat16 [384, 384], replicated, may hold values from -0.3125 to 0.3125
- w_out: bfloat16 [384, 384], replicated, may hold values from -2.5 to 2.5
- w_bias: bfloat16 [128, 16], replicated, may hold values from -0.5 to 0.5
- rel_table: bfloat16 [66, 128], replicated, may hold values from -6 to 6
- w_mix_a: bfloat16 [384, 128], replicated, may hold values from -0.3125 to 0.3125
- w_mix_b: bfloat16 [384, 128], replicated, may hold values from -0.3125 to 0.3125
- w_hidden_a: bfloat16 [128, 512], replicated, may hold values from -0.5 to 0.5
- w_hidden_b: bfloat16 [128, 512], replicated, may hold values from -0.5 to 0.5
- w_hidden_out: bfloat16 [512, 128], replicated, may hold values from -0.25 to 0.25
- w_pae: bfloat16 [128, 64], replicated, may hold values from -30 to 30
- pae_bias: float32 [64], replicated, may hold values from -4 to 4
Outputs:
- refined: bfloat16 [256, 384], P(('groups', 'rows')), parts along dimension 0
- errors: float32 [256, 128], P(('groups', 'rows')), parts along dimension 0
There are 2 independent parts, one for each index of `groups`. A program takes and returns all parts, laid end to end along the dimension named above; an argument that names none is the same for every part. Nothing has to cross between parts.
Inputs may be any that keep to these rules, and one draw needn't show every extreme that they name: `complex_index`: never falls along the tokens; each complex holds 1 to 96 consecutive tokens.
All inputs are finite; a program needn't handle non-finite values.
Results may differ from a plain program's by a relative error of at most 0.023.
Values may be sent and summed in bfloat16 or wider, within the bound.
A program may use at most 128 MiB of HBM per device.

v0:
```python
import functools
import math

import jax
import jax.numpy as jnp
from jax import lax
from jax.experimental import pallas as pl
from jax.experimental.pallas import tpu as pltpu
from jax.sharding import PartitionSpec as P

epsilon = 1e-05
masked_score = -1e30
chain_step = 65536.0
f32 = jnp.float32
bf16 = jnp.bfloat16


def norm_rows(values):
    center = values - jnp.mean(values, axis=-1, keepdims=True)
    spread = jnp.mean(center * center, axis=-1, keepdims=True)
    return center * lax.rsqrt(spread + epsilon)


def mm(a, b):
    return jnp.dot(a, b, preferred_element_type=f32)


def mm_nt(a, b):
    return lax.dot_general(a, b, (((1,), (1,)), ((), ())), preferred_element_type=f32)


def column(row):
    m = row.shape[1]
    pick = lax.broadcasted_iota(jnp.int32, (m, m), 0) == lax.broadcasted_iota(jnp.int32, (m, m), 1)
    return jnp.sum(jnp.where(pick, row, 0.0), axis=1, keepdims=True)


def bucket_onehot(diff, classes):
    reach = (classes - 2) // 2
    same = jnp.abs(diff) < 0.5 * chain_step
    bucket = jnp.where(same, jnp.clip(diff, -reach, reach) + reach, 2.0 * reach + 1.0)
    lanes = lax.broadcasted_iota(jnp.int32, bucket.shape, bucket.ndim - 1).astype(f32)
    return jnp.where(bucket == lanes, 1.0, 0.0).astype(bf16)


def kernel(
    n,
    heads,
    pair_h, single_h, res_h, chain_h, complex_h, pad_h,
    wq_h, wk_h, wv_h, wg_h, wo_h, wb_h, rel_h, wma_h, wmb_h, wha_h, whb_h, who_h, wp_h, pb_h,
    refined_ref, errors_ref,
    pair_v, single_v, res_v, chain_v, complex_v, pad_v,
    wq_v, wk_v, wv_v, wg_v, wo_v, wb_v, rel_v, wma_v, wmb_v, wha_v, whb_v, who_v, wp_v, pb_v,
    code_v, ccol_v, bias_s, bias_r, single_r, pair_r, b_s, b_r, a_v, pin_v, score_v,
    local_sem, own_sem, send_sem, recv_sem,
):
    me = lax.axis_index("rows")
    count, rows, width = pair_h.shape
    classes = rel_h.shape[0]
    inner = single_h.shape[1]
    head_size = inner // heads
    first = pl.multiple_of(me * rows, rows)

    hbm = (pair_h, single_h, res_h, chain_h, complex_h, pad_h, wq_h, wk_h, wv_h, wg_h, wo_h,
           wb_h, rel_h, wma_h, wmb_h, wha_h, whb_h, who_h, wp_h, pb_h)
    vmem = (pair_v, single_v, res_v, chain_v, complex_v, pad_v, wq_v, wk_v, wv_v, wg_v, wo_v,
            wb_v, rel_v, wma_v, wmb_v, wha_v, whb_v, who_v, wp_v, pb_v)
    (PAIR, SINGLE, RES, CHAIN, COMPLEX, PAD, WQ, WK, WV, WG, WO, WB, REL, WMA, WMB, WHA, WHB,
     WHO, WP, PB) = range(len(hbm))
    loads = [pltpu.make_async_copy(h, v, local_sem.at[i]) for i, (h, v) in enumerate(zip(hbm, vmem))]

    barrier = pltpu.get_barrier_semaphore()

    def greet(s, _):
        pl.semaphore_signal(
            barrier, inc=1, device_id={"rows": lax.rem(me + s, n)},
            device_id_type=pl.DeviceIdType.MESH,
        )
        return 0

    lax.fori_loop(1, n, greet, 0)
    for i in (RES, CHAIN, REL, WB, PAIR, SINGLE, COMPLEX, PAD, WQ, WG, WK, WV, WO, WMB, WMA,
              WHA, WHB, WHO, WP, PB):
        loads[i].start()

    for i in (RES, CHAIN, COMPLEX):
        loads[i].wait()
    step = min(count, 128)
    for k in range(0, count, step):
        code = chain_v[:, k:k + step].astype(f32) * chain_step + res_v[:, k:k + step].astype(f32)
        code_v[k:k + step, :] = jnp.broadcast_to(column(code), (step, 128))
        ccol_v[k:k + step, :] = jnp.broadcast_to(
            column(complex_v[:, k:k + step].astype(f32)), (step, 128))

    for i in (REL, WB, PAIR):
        loads[i].wait()
    rel = rel_v[...]
    spots = rows * heads
    tile_h = jnp.where(
        lax.broadcasted_iota(jnp.int32, (heads, spots), 1) % heads
        == lax.broadcasted_iota(jnp.int32, (heads, spots), 0), 1.0, 0.0).astype(bf16)
    w_tiled = lax.dot_general(
        wb_v[...], tile_h, (((0,), (0,)), ((), ())), preferred_element_type=f32).astype(bf16)
    code_keys = code_v[pl.ds(first, rows), :classes]

    def bias_block(j, _):
        at = pl.multiple_of(j * step, step)
        code_i = code_v[pl.ds(at, step), :classes]
        diff = code_i[:, None, :] - code_keys[None, :, :]
        hot = bucket_onehot(diff.reshape(step * rows, classes), classes)
        cells = mm(hot, rel) + pair_v[pl.ds(at, step)].astype(f32).reshape(step * rows, width)
        out = mm(norm_rows(cells).astype(bf16), w_tiled)
        out = out.reshape(step // rows, rows, rows, spots)
        lane_q = lax.broadcasted_iota(jnp.int32, (1, 1, spots), 2) // heads
        total = jnp.where(lane_q == 0, out[:, 0], 0.0)
        for q in range(1, rows):
            total = jnp.where(lane_q == q, out[:, q], total)
        bias_s[pl.ds(pl.multiple_of(j * (step // rows), step // rows), step // rows)] = total.astype(bf16)
        return 0

    lax.fori_loop(0, count // step, bias_block, 0, unroll=count == step)
    loads[SINGLE].wait()

    pl.semaphore_wait(barrier, n - 1)

    def remote(src, dst, i, peer):
        return pltpu.make_async_remote_copy(
            src_ref=src, dst_ref=dst, send_sem=send_sem.at[i], recv_sem=recv_sem.at[i],
            device_id={"rows": peer}, device_id_type=pl.DeviceIdType.MESH)

    def send_single(s, _):
        peer = lax.rem(me + s, n)
        remote(single_v, single_r.at[me], 0, peer).start()
        return 0

    def send_bias(s, _):
        peer = lax.rem(me + s, n)
        remote(bias_s.at[peer], bias_r.at[me], 1, peer).start()
        return 0

    def send_pair(s, _):
        peer = lax.rem(me + s, n)
        remote(pair_v.at[pl.ds(peer * rows, rows)], pair_r.at[:, me], 2, peer).start()
        return 0

    lax.fori_loop(1, n, send_single, 0)
    lax.fori_loop(1, n, send_bias, 0)
    lax.fori_loop(1, n, send_pair, 0)
    own = (
        pltpu.make_async_copy(single_v, single_r.at[me], own_sem.at[0]),
        pltpu.make_async_copy(bias_s.at[me], bias_r.at[me], own_sem.at[1]),
        pltpu.make_async_copy(pair_v.at[pl.ds(first, rows)], pair_r.at[:, me], own_sem.at[2]),
    )
    for copy in own:
        copy.start()

    mine = single_v[...].astype(f32)
    normed = norm_rows(mine).astype(bf16)
    loads[WQ].wait()
    queries = mm(normed, wq_v[...]).astype(bf16).astype(f32)
    loads[WG].wait()
    gating = jax.nn.sigmoid(mm(normed, wg_v[...]))
    head_of = lax.broadcasted_iota(jnp.int32, (heads, inner), 1) // head_size
    own_head = head_of == lax.broadcasted_iota(jnp.int32, (heads, inner), 0)
    q_wide = jnp.concatenate(
        [jnp.where(own_head, queries[q:q + 1, :], 0.0) for q in range(rows)], axis=0).astype(bf16)

    def rel_block(q, _):
        diff = code_v[pl.ds(first + q, 1), :classes] - code_v[:, :classes]
        pin_v[q] = mm(bucket_onehot(diff, classes), rel)
        return 0

    lax.fori_loop(0, rows, rel_block, 0, unroll=count == step)

    loads[WK].wait()
    loads[WV].wait()
    own[0].wait()
    landed = single_r.at[pl.ds(0, n - 1)]
    pltpu.make_async_copy(landed, landed, recv_sem.at[0]).wait()
    every = norm_rows(single_r[...].astype(f32).reshape(count, inner)).astype(bf16)
    keys = mm(every, wk_v[...]).astype(bf16)
    values = mm(every, wv_v[...]).astype(bf16)
    scores = mm_nt(q_wide, keys) / math.sqrt(head_size)
    loads[PAD].wait()
    key_ids = lax.broadcasted_iota(jnp.int32, (1, count), 1)
    complex_row = complex_v[...].astype(f32)
    real = pad_v[...] == 1
    own[1].wait()
    landed = bias_r.at[pl.ds(0, n - 1)]
    pltpu.make_async_copy(landed, landed, recv_sem.at[1]).wait()
    eye = jnp.where(
        lax.broadcasted_iota(jnp.int32, (spots, spots), 0)
        == lax.broadcasted_iota(jnp.int32, (spots, spots), 1), 1.0, 0.0).astype(bf16)
    arrived = bias_r[...].astype(f32).reshape(count, spots).astype(bf16)
    scores = scores + mm_nt(eye, arrived)
    for q in range(rows):
        allowed = (ccol_v[pl.ds(first + q, 1), 0:1] == complex_row) & (real | (key_ids == first + q))
        part = scores[q * heads:(q + 1) * heads, :]
        score_v[q * heads:(q + 1) * heads, :] = jnp.where(allowed, part, masked_score)
    scores = score_v[...]
    expo = jnp.exp(scores - jnp.max(scores, axis=-1, keepdims=True))
    total = jnp.sum(expo, axis=-1, keepdims=True)
    mixed_heads = mm(expo.astype(bf16), values) / total
    attended = jnp.concatenate(
        [jnp.sum(jnp.where(own_head, mixed_heads[q * heads:(q + 1) * heads, :], 0.0),
                 axis=0, keepdims=True) for q in range(rows)], axis=0)
    loads[WO].wait()
    refined = (mine + mm((gating * attended).astype(bf16), wo_v[...])).astype(bf16)
    renormed = norm_rows(refined.astype(f32)).astype(bf16)
    loads[WMB].wait()
    b_s[...] = mm(renormed, wmb_v[...]).astype(bf16)
    b_r[me] = b_s[...]
    loads[WMA].wait()
    a_v[...] = mm(renormed, wma_v[...]).astype(bf16).astype(f32)

    def send_b(s, _):
        remote(b_s, b_r.at[me], 3, lax.rem(me + s, n)).start()
        return 0

    lax.fori_loop(1, n, send_b, 0)
    refined_ref[...] = refined

    own[2].wait()
    landed = pair_r.at[:, pl.ds(0, n - 1)]
    pltpu.make_async_copy(landed, landed, recv_sem.at[2]).wait()

    def add_block(q, _):
        pin_v[q] = pin_v[q] + pair_r[q].astype(f32).reshape(count, width)
        return 0

    lax.fori_loop(0, rows, add_block, 0, unroll=count == step)
    for i in (WHA, WHB, WHO, WP, PB):
        loads[i].wait()
    bins = wp_v.shape[0]
    bias_col = column(pb_v[...])
    centers = (lax.broadcasted_iota(jnp.int32, (bins, 1), 0).astype(f32) + 0.5) * (32.0 / bins)
    landed = b_r.at[pl.ds(0, n - 1)]
    pltpu.make_async_copy(landed, landed, recv_sem.at[3]).wait()

    def tail(c, _):
        at = pl.multiple_of(c * step, step)
        tile = pl.multiple_of(c * (step // rows), step // rows)
        factor_b = b_r[pl.ds(tile, step // rows)].astype(f32).reshape(step, width)
        found = []
        for q in range(rows):
            flat = pin_v[q, pl.ds(at, step), :] + a_v[q:q + 1, :] * factor_b
            x = norm_rows(flat).astype(bf16)
            gate = mm(x, wha_v[...])
            up = mm(x, whb_v[...])
            half = 0.5 * gate
            hidden = ((half + half * jnp.tanh(half)) * up).astype(bf16)
            updated = flat + mm(hidden, who_v[...])
            final = norm_rows(updated).astype(bf16)
            logits = mm_nt(wp_v[...], final) + bias_col
            expo = jnp.exp(logits - jnp.max(logits, axis=0, keepdims=True))
            found.append(jnp.sum(expo * centers, axis=0, keepdims=True)
                         / jnp.sum(expo, axis=0, keepdims=True))
        errors_ref[:, pl.ds(at, step)] = jnp.concatenate(found, axis=0)
        return 0

    lax.fori_loop(0, count // step, tail, 0, unroll=count == step)

    for i, buf in enumerate((single_r, bias_r, None, b_r)):
        sent = pair_r.at[:, pl.ds(0, n - 1)] if buf is None else buf.at[pl.ds(0, n - 1)]
        pltpu.make_async_copy(sent, sent, send_sem.at[i]).wait()


def on_device(n, pair_repr, single_repr, residue_index, chain_index, complex_index, pad_mask,
              w_query, w_key, w_value, w_gate, w_out, w_bias, rel_table, w_mix_a, w_mix_b,
              w_hidden_a, w_hidden_b, w_hidden_out, w_pae, pae_bias):
    count, rows, width = pair_repr.shape
    inner = single_repr.shape[1]
    heads = w_bias.shape[1]
    args = (pair_repr, single_repr, residue_index[None], chain_index[None], complex_index[None],
            pad_mask[None], w_query, w_key, w_value, w_gate, w_out, w_bias.T, rel_table,
            w_mix_a, w_mix_b, w_hidden_a, w_hidden_b, w_hidden_out, w_pae.T, pae_bias[None])
    spots = rows * heads
    scratch = [pltpu.VMEM(a.shape, a.dtype) for a in args] + [
        pltpu.VMEM((count, 128), f32),
        pltpu.VMEM((count, 128), f32),
        pltpu.VMEM((n, rows, spots), bf16),
        pltpu.VMEM((n, rows, spots), bf16),
        pltpu.VMEM((n, rows, inner), bf16),
        pltpu.VMEM((rows, n, rows, width), bf16),
        pltpu.VMEM((rows, width), bf16),
        pltpu.VMEM((n, rows, width), bf16),
        pltpu.VMEM((rows, width), f32),
        pltpu.VMEM((rows, count, width), f32),
        pltpu.VMEM((spots, count), f32),
        pltpu.SemaphoreType.DMA((len(args),)),
        pltpu.SemaphoreType.DMA((3,)),
        pltpu.SemaphoreType.DMA((4,)),
        pltpu.SemaphoreType.DMA((4,)),
    ]
    return pl.pallas_call(
        functools.partial(kernel, n, heads),
        out_shape=(
            jax.ShapeDtypeStruct((rows, inner), bf16),
            jax.ShapeDtypeStruct((rows, count), f32),
        ),
        in_specs=[pl.BlockSpec(memory_space=pltpu.HBM)] * len(args),
        out_specs=[pl.BlockSpec(memory_space=pltpu.VMEM)] * 2,
        scratch_shapes=scratch,
        compiler_params=pltpu.CompilerParams(
            collective_id=0, has_side_effects=True, vmem_limit_bytes=60 * 1024 * 1024),
        name="confidence",
    )(*args)


def solution(mesh):
    placed = (
        P("groups", "rows", None),
        P(("groups", "rows"), None),
        P("groups"),
        P("groups"),
        P("groups"),
        P("groups"),
    ) + (P(),) * 14
    return jax.shard_map(
        functools.partial(on_device, mesh.shape["rows"]),
        mesh=mesh,
        in_specs=placed,
        out_specs=(P(("groups", "rows"), None), P(("groups", "rows"), None)),
        check_vma=False,
    )
```

profile of v0, /device:TPU:0, one launch (start us, length us, event | category | flops | bytes accessed | tf_op | source)
XLA Modules:
  0.0 25.8 jit_solution(6184261201672486467)
XLA Ops:
  0.6 23.3 %confidence.1 = (bf16[8,384]{1,0:T(8,128)(2,1)}, f32[8,128]{1,0:T(8,128)}) custom-call(bf16[128,8,128]{2,1,0:T(8,128)(2,1)} %pair_h.1, bf16[8,384]{1,0:T(8,128)(2,1)} %single_h.1, s32[1,128]{1,0:T(1,128)} %bitcast.9, s32[1,128]{1,0:T(1,128)} %bitcast.10, s32[1,128]{1,0:T(1,128)} %bitcast.11, s32[1,128]{1,0:T(1,128)} %bitcast.12, bf16[384,384]{1,0:T(8,128)(2,1)} %wq_h.1, ...), custom_call_target="tpu_custom_call" | custom-call | tf_op jit(solution)/shard_map/confidence/pallas_call | solution.py:295
  23.9 0.0 copy-start
  23.9 1.3 %copy.24 = bf16[8,384]{1,0:T(8,128)(2,1)} copy(bf16[8,384]{1,0:T(8,128)(2,1)} %get-tuple-element.4) | data formatting | bytes 12288
  25.2 0.0 copy-done
  25.2 0.6 %copy.25 = f32[8,128]{1,0:T(8,128)} copy(f32[8,128]{1,0:T(8,128)S(1)} %copy-done) | data formatting | bytes 8192
Async XLA Ops:
  23.9 1.3 %copy-start = (f32[8,128]{1,0:T(8,128)S(1)}, f32[8,128]{1,0:T(8,128)}, u32[]{:S(2)}) copy-start(f32[8,128]{1,0:T(8,128)} %get-tuple-element.5) | copy-start | bytes 12292
where the time goes:
time: 26 us; the launch traced here: 25.8 us
  Pallas kernels  23.3 us (90%)
  local copies, waits for them, and re-layouts  1.88 us (7%)
  between operations  0.66 us (3%)
    pallas_call x1, Pallas kernels, on_device(): pl.pallas_call(functools.partial(kernel, n, heads), out_shape=(jax.ShapeD...  23.3 us
    unnamed x4, local copies, waits for them, and re-layouts  1.88 us

commit v1 on v0

v1 whole, which is shorter than its diff:
```python
import functools
import math

import jax
import jax.numpy as jnp
from jax import lax
from jax.experimental import pallas as pl
from jax.experimental.pallas import tpu as pltpu
from jax.sharding import PartitionSpec as P

epsilon = 1e-05
masked_score = -1e30
chain_step = 65536.0
f32 = jnp.float32
bf16 = jnp.bfloat16


def norm_rows(values):
    center = values - jnp.mean(values, axis=-1, keepdims=True)
    spread = jnp.mean(center * center, axis=-1, keepdims=True)
    return center * lax.rsqrt(spread + epsilon)


def mm(a, b):
    return jnp.dot(a, b, preferred_element_type=f32)


def mm_nt(a, b):
    return lax.dot_general(a, b, (((1,), (1,)), ((), ())), preferred_element_type=f32)


def mm_tn(a, b):
    return lax.dot_general(a, b, (((0,), (0,)), ((), ())), preferred_element_type=f32)


def column(row):
    m = row.shape[1]
    pick = lax.broadcasted_iota(jnp.int32, (m, m), 0) == lax.broadcasted_iota(jnp.int32, (m, m), 1)
    return jnp.sum(jnp.where(pick, row, 0.0), axis=1, keepdims=True)


def bucket_onehot(diff, classes):
    reach = (classes - 2) // 2
    same = jnp.abs(diff) < 0.5 * chain_step
    bucket = jnp.where(same, jnp.clip(diff, -reach, reach) + reach, 2.0 * reach + 1.0)
    lanes = lax.broadcasted_iota(jnp.int32, bucket.shape, bucket.ndim - 1).astype(f32)
    return jnp.where(bucket == lanes, 1.0, 0.0).astype(bf16)


def kernel(
    n,
    heads,
    pair_h, single_h, res_h, chain_h, complex_h, pad_h,
    wq_h, wk_h, wv_h, wg_h, wo_h, wb_h, rel_h, wma_h, wmb_h, wha_h, whb_h, who_h, wp_h, pb_h,
    refined_ref, errors_ref,
    pair_v, single_v, res_v, chain_v, complex_v, pad_v,
    wq_v, wk_v, wv_v, wg_v, wo_v, wb_v, rel_v, wma_v, wmb_v, wha_v, whb_v, who_v, wp_v, pb_v,
    code_v, ccol_v, mask_v, bias_s, bias_r, norm_s, norm_r, pair_r, b_s, b_r, a_v, pin_v,
    flat_v, x_v, hid_v,
    local_sem, send_sem, recv_sem,
):
    me = lax.axis_index("rows")
    count, rows, width = pair_h.shape
    classes = rel_h.shape[0]
    inner = single_h.shape[1]
    head_size = inner // heads
    spots = rows * heads
    first = pl.multiple_of(me * rows, rows)
    step = min(count, 128)
    short = count == step

    hbm = (pair_h, single_h, res_h, chain_h, complex_h, pad_h, wq_h, wk_h, wv_h, wg_h, wo_h,
           wb_h, rel_h, wma_h, wmb_h, wha_h, whb_h, who_h, wp_h, pb_h)
    vmem = (pair_v, single_v, res_v, chain_v, complex_v, pad_v, wq_v, wk_v, wv_v, wg_v, wo_v,
            wb_v, rel_v, wma_v, wmb_v, wha_v, whb_v, who_v, wp_v, pb_v)
    (PAIR, SINGLE, RES, CHAIN, COMPLEX, PAD, WQ, WK, WV, WG, WO, WB, REL, WMA, WMB, WHA, WHB,
     WHO, WP, PB) = range(len(hbm))
    loads = [pltpu.make_async_copy(h, v, local_sem.at[i]) for i, (h, v) in enumerate(zip(hbm, vmem))]

    def arrive(*which):
        for i in which:
            loads[i].wait()

    bits = n.bit_length() - 1
    flips = [(1 << b) * (1 - 2 * ((me // (1 << b)) % 2)) for b in range(bits)]

    def each_peer(visit):
        if short and n == 1 << bits:
            for s in reversed(range(1, n)):
                visit(me + sum(flips[b] for b in range(bits) if s >> b & 1))
        else:
            def body(s, _):
                visit(lax.rem(me + s, n))
                return 0

            lax.fori_loop(1, n, body, 0)

    for i in (RES, CHAIN, SINGLE):
        loads[i].start()
    barrier = pltpu.get_barrier_semaphore()
    each_peer(lambda peer: pl.semaphore_signal(
        barrier, inc=1, device_id={"rows": peer}, device_id_type=pl.DeviceIdType.MESH))
    for i in (REL, WB, PAIR, COMPLEX, PAD, WQ, WG, WK, WV, WO, WMB, WMA, WHA, WHB, WHO, WP, PB):
        loads[i].start()

    arrive(RES, CHAIN)
    for k in range(0, count, step):
        code = chain_v[:, k:k + step].astype(f32) * chain_step + res_v[:, k:k + step].astype(f32)
        code_v[k:k + step, :] = jnp.broadcast_to(column(code), (step, 128))

    arrive(SINGLE)
    mine = single_v[...].astype(f32)
    normed = norm_rows(mine).astype(bf16)
    norm_s[...] = normed
    norm_r[me] = normed

    arrive(REL, WB, PAIR)
    rel = rel_v[...]
    tile_h = jnp.where(
        lax.broadcasted_iota(jnp.int32, (heads, spots), 1) % heads
        == lax.broadcasted_iota(jnp.int32, (heads, spots), 0), 1.0, 0.0).astype(bf16)
    w_tiled = mm_tn(wb_v[...], tile_h).astype(bf16)
    code_keys = code_v[pl.ds(first, rows), :classes]

    def bias_block(j, _):
        at = pl.multiple_of(j * step, step)
        code_i = code_v[pl.ds(at, step), :classes]
        diff = code_i[:, None, :] - code_keys[None, :, :]
        hot = bucket_onehot(diff.reshape(step * rows, classes), classes)
        cells = mm(hot, rel) + pair_v[pl.ds(at, step)].astype(f32).reshape(step * rows, width)
        out = mm(norm_rows(cells).astype(bf16), w_tiled)
        out = out.reshape(step // rows, rows, rows, spots)
        lane_q = lax.broadcasted_iota(jnp.int32, (1, 1, spots), 2) // heads
        total = jnp.where(lane_q == 0, out[:, 0], 0.0)
        for q in range(1, rows):
            total = jnp.where(lane_q == q, out[:, q], total)
        bias_s[pl.ds(pl.multiple_of(j * (step // rows), step // rows), step // rows)] = total.astype(bf16)
        return 0

    lax.fori_loop(0, count // step, bias_block, 0, unroll=short)
    bias_r[me] = bias_s[me]

    pl.semaphore_wait(barrier, n - 1)

    def remote(src, dst, i, peer):
        return pltpu.make_async_remote_copy(
            src_ref=src, dst_ref=dst, send_sem=send_sem.at[i], recv_sem=recv_sem.at[i],
            device_id={"rows": peer}, device_id_type=pl.DeviceIdType.MESH)

    each_peer(lambda peer: remote(norm_s, norm_r.at[me], 0, peer).start())
    each_peer(lambda peer: remote(bias_s.at[peer], bias_r.at[me], 1, peer).start())

    arrive(WQ)
    queries = mm(normed, wq_v[...]).astype(bf16).astype(f32)
    arrive(WG)
    gating = jax.nn.sigmoid(mm(normed, wg_v[...]))
    head_of = lax.broadcasted_iota(jnp.int32, (heads, inner), 1) // head_size
    own_head = head_of == lax.broadcasted_iota(jnp.int32, (heads, inner), 0)
    q_wide = jnp.concatenate(
        [jnp.where(own_head, queries[q:q + 1, :], 0.0) for q in range(rows)], axis=0).astype(bf16)
    arrive(WK)
    toward = (mm_nt(wk_v[...], q_wide) / math.sqrt(head_size)).astype(bf16)

    each_peer(lambda peer: remote(
        pair_v.at[pl.ds(peer * rows, rows)], pair_r.at[me], 2, peer).start())
    pair_r[me] = pair_v[pl.ds(first, rows)]

    arrive(COMPLEX, PAD)
    lane_spot = lax.broadcasted_iota(jnp.int32, (step, spots), 1) // heads
    for k in range(0, count, step):
        ccol_v[k:k + step, :] = jnp.broadcast_to(
            column(complex_v[:, k:k + step].astype(f32)), (step, 128))
    mine_c = ccol_v[pl.ds(first, rows), 0:1]
    lane_row = lax.broadcasted_iota(jnp.int32, (rows, spots), 1) // heads
    pick = lane_row == lax.broadcasted_iota(jnp.int32, (rows, spots), 0)
    query_c = jnp.sum(jnp.where(pick, mine_c, 0.0), axis=0, keepdims=True)
    for k in range(0, count, step):
        real = column(pad_v[:, k:k + step].astype(f32)) == 1.0
        same = ccol_v[k:k + step, :spots] == query_c
        itself = (lax.broadcasted_iota(jnp.int32, (step, spots), 0) + k) == (first + lane_spot)
        mask_v[k:k + step, :] = jnp.where(same & (real | itself), 0.0, masked_score)

    def rel_block(q, _):
        diff = code_v[pl.ds(first + q, 1), :classes] - code_v[:, :classes]
        pin_v[q] = mm(bucket_onehot(diff, classes), rel)
        return 0

    lax.fori_loop(0, rows, rel_block, 0, unroll=short)

    arrive(WHA, WHB, WHO, WP, PB)
    wha_v[...] = (wha_v[...].astype(f32) * 0.5).astype(bf16)
    bins = wp_v.shape[0]
    bias_col = column(pb_v[...])
    centers = (lax.broadcasted_iota(jnp.int32, (bins, 1), 0).astype(f32) + 0.5) * (32.0 / bins)
    arrive(WV, WO, WMB, WMA)

    landed = norm_r.at[pl.ds(0, n - 1)]
    pltpu.make_async_copy(landed, landed, recv_sem.at[0]).wait()
    every = norm_r[...].astype(f32).reshape(count, inner).astype(bf16)
    scores = mm(every, toward)
    values = mm(every, wv_v[...]).astype(bf16)
    landed = bias_r.at[pl.ds(0, n - 1)]
    pltpu.make_async_copy(landed, landed, recv_sem.at[1]).wait()
    scores = scores + bias_r[...].astype(f32).reshape(count, spots) + mask_v[...]
    expo = jnp.exp(scores - jnp.max(scores, axis=0, keepdims=True))
    weights = (expo * (1.0 / jnp.sum(expo, axis=0, keepdims=True))).astype(bf16)
    mixed_heads = mm_tn(weights, values)
    attended = jnp.concatenate(
        [jnp.sum(jnp.where(own_head, mixed_heads[q * heads:(q + 1) * heads, :], 0.0),
                 axis=0, keepdims=True) for q in range(rows)], axis=0)
    refined = (mine + mm((gating * attended).astype(bf16), wo_v[...])).astype(bf16)
    renormed = norm_rows(refined.astype(f32)).astype(bf16)
    factor_b = mm(renormed, wmb_v[...]).astype(bf16)
    b_s[...] = factor_b
    a_v[...] = mm(renormed, wma_v[...]).astype(bf16).astype(f32)
    b_r[me] = factor_b
    refined_ref[...] = refined

    each_peer(lambda peer: remote(b_s, b_r.at[me], 3, peer).start())

    landed = pair_r.at[pl.ds(0, n - 1)]
    pltpu.make_async_copy(landed, landed, recv_sem.at[2]).wait()

    def add_block(q, _):
        pin_v[q] = pin_v[q] + pair_r[:, q].astype(f32).reshape(count, width)
        return 0

    lax.fori_loop(0, rows, add_block, 0, unroll=short)

    landed = b_r.at[pl.ds(0, n - 1)]
    pltpu.make_async_copy(landed, landed, recv_sem.at[3]).wait()

    def tail(c, _):
        at = pl.multiple_of(c * step, step)
        tile = pl.multiple_of(c * (step // rows), step // rows)
        factor_b = b_r[pl.ds(tile, step // rows)].astype(f32).reshape(step, width)
        for q in range(rows):
            flat = pin_v[q, pl.ds(at, step), :] + a_v[q:q + 1, :] * factor_b
            flat_v[q * step:(q + 1) * step, :] = flat
            x_v[q * step:(q + 1) * step, :] = norm_rows(flat).astype(bf16)
        cut = 256
        for k in range(0, wha_v.shape[1], cut):
            wa = wha_v[:, k:k + cut]
            wb = whb_v[:, k:k + cut]
            for q in range(rows):
                x = x_v[q * step:(q + 1) * step, :]
                half = mm(x, wa)
                up = mm(x, wb)
                hid_v[q * step:(q + 1) * step, k:k + cut] = (
                    (half + half * jnp.tanh(half)) * up).astype(bf16)
        for q in range(rows):
            updated = flat_v[q * step:(q + 1) * step, :] + mm(hid_v[q * step:(q + 1) * step, :], who_v[...])
            x_v[q * step:(q + 1) * step, :] = norm_rows(updated).astype(bf16)
        found = []
        for q in range(rows):
            logits = mm_nt(wp_v[...], x_v[q * step:(q + 1) * step, :]) + bias_col
            expo = jnp.exp(logits - jnp.max(logits, axis=0, keepdims=True))
            found.append(jnp.sum(expo * centers, axis=0, keepdims=True)
                         / jnp.sum(expo, axis=0, keepdims=True))
        errors_ref[:, pl.ds(at, step)] = jnp.concatenate(found, axis=0)
        return 0

    lax.fori_loop(0, count // step, tail, 0, unroll=short)

    for i, buf in enumerate((norm_r, bias_r, pair_r, b_r)):
        sent = buf.at[pl.ds(0, n - 1)]
        pltpu.make_async_copy(sent, sent, send_sem.at[i]).wait()


def place(refined_v, errors_v, refined_h, errors_h, sem):
    copies = (
        pltpu.make_async_copy(refined_v, refined_h, sem.at[0]),
        pltpu.make_async_copy(errors_v, errors_h, sem.at[1]),
    )
    for copy in copies:
        copy.start()
    for copy in copies:
        copy.wait()


def on_device(n, pair_repr, single_repr, residue_index, chain_index, complex_index, pad_mask,
              w_query, w_key, w_value, w_gate, w_out, w_bias, rel_table, w_mix_a, w_mix_b,
              w_hidden_a, w_hidden_b, w_hidden_out, w_pae, pae_bias):
    count, rows, width = pair_repr.shape
    inner = single_repr.shape[1]
    heads = w_bias.shape[1]
    hidden = w_hidden_a.shape[1]
    args = (pair_repr, single_repr, residue_index[None], chain_index[None], complex_index[None],
            pad_mask[None], w_query, w_key, w_value, w_gate, w_out, w_bias.T, rel_table,
            w_mix_a, w_mix_b, w_hidden_a, w_hidden_b, w_hidden_out, w_pae.T, pae_bias[None])
    spots = rows * heads
    step = min(count, 128)
    scratch = [pltpu.VMEM(a.shape, a.dtype) for a in args] + [
        pltpu.VMEM((count, 128), f32),
        pltpu.VMEM((count, 128), f32),
        pltpu.VMEM((count, spots), f32),
        pltpu.VMEM((n, rows, spots), bf16),
        pltpu.VMEM((n, rows, spots), bf16),
        pltpu.VMEM((rows, inner), bf16),
        pltpu.VMEM((n, rows, inner), bf16),
        pltpu.VMEM((n, rows, rows, width), bf16),
        pltpu.VMEM((rows, width), bf16),
        pltpu.VMEM((n, rows, width), bf16),
        pltpu.VMEM((rows, width), f32),
        pltpu.VMEM((rows, count, width), f32),
        pltpu.VMEM((rows * step, width), f32),
        pltpu.VMEM((rows * step, width), bf16),
        pltpu.VMEM((rows * step, hidden), bf16),
        pltpu.SemaphoreType.DMA((len(args),)),
        pltpu.SemaphoreType.DMA((4,)),
        pltpu.SemaphoreType.DMA((4,)),
    ]
    refined, errors = pl.pallas_call(
        functools.partial(kernel, n, heads),
        out_shape=(pltpu.VMEM((rows, inner), bf16), pltpu.VMEM((rows, count), f32)),
        in_specs=[pl.BlockSpec(memory_space=pltpu.HBM)] * len(args),
        out_specs=[pl.BlockSpec(memory_space=pltpu.VMEM)] * 2,
        scratch_shapes=scratch,
        compiler_params=pltpu.CompilerParams(
            collective_id=0, has_side_effects=True, vmem_limit_bytes=40 * 1024 * 1024),
        name="confidence",
    )(*[pltpu.with_memory_space_constraint(a, pltpu.HBM) for a in args])
    return pl.pallas_call(
        place,
        out_shape=(
            jax.ShapeDtypeStruct((rows, inner), bf16),
            jax.ShapeDtypeStruct((rows, count), f32),
        ),
        in_specs=[pl.BlockSpec(memory_space=pltpu.VMEM)] * 2,
        out_specs=[pl.BlockSpec(memory_space=pltpu.HBM)] * 2,
        scratch_shapes=[pltpu.SemaphoreType.DMA((2,))],
        compiler_params=pltpu.CompilerParams(vmem_limit_bytes=1024 * 1024),
        name="place",
    )(refined, errors)


def solution(mesh):
    placed = (
        P("groups", "rows", None),
        P(("groups", "rows"), None),
        P("groups"),
        P("groups"),
        P("groups"),
        P("groups"),
    ) + (P(),) * 14
    return jax.shard_map(
        functools.partial(on_device, mesh.shape["rows"]),
        mesh=mesh,
        in_specs=placed,
        out_specs=(P(("groups", "rows"), None), P(("groups", "rows"), None)),
        check_vma=False,
    )
```

time: 26 us -> 22.8 us (0.88)
  local copies, waits for them, and re-layouts: 1.88 us -> 0 us
  Pallas kernels: 23.3 us -> 22 us
    unnamed x4 -> x0, local copies, waits for them, and re-layouts: 1.88 us -> none
    pallas_call x1 -> x2, Pallas kernels: 23.3 us -> 22 us  [the longest x1 21.4 us: on_device(): pl.pallas_call(functools.partial(kernel, n, heads), out_shape=(pltpu.VMEM...]
where the time goes in v1:
time: 22.8 us; the launch traced here: 22.7 us
  Pallas kernels  22 us (96%)
  between operations  0.65 us (3%)
    pallas_call x1, Pallas kernels, on_device(): pl.pallas_call(functools.partial(kernel, n, heads), out_shape=(pltpu.VMEM...  21.4 us
    pallas_call x1, Pallas kernels, on_device(): pl.pallas_call(place, out_shape=(jax.ShapeDtypeStruct((rows, inner), bf16...  0.62 us

profile of v1, /device:TPU:0, one launch (start us, length us, event | category | flops | bytes accessed | tf_op | source)
XLA Modules:
  0.0 22.7 jit_solution(18314050579622541301)
XLA Ops:
  0.6 21.4 %confidence.1 = (bf16[8,384]{1,0:T(8,128)(2,1)S(1)}, f32[8,128]{1,0:T(8,128)S(1)}) custom-call(bf16[128,8,128]{2,1,0:T(8,128)(2,1)} %pair_h.1, bf16[8,384]{1,0:T(8,128)(2,1)} %single_h.1, s32[1,128]{1,0:T(1,128)} %bitcast.9, s32[1,128]{1,0:T(1,128)} %bitcast.10, s32[1,128]{1,0:T(1,128)} %bitcast.11, s32[1,128]{1,0:T(1,128)} %bitcast.12, ...), custom_call_target="tpu_custom_call" | custom-call | tf_op jit(solution)/shard_map/confidence/pallas_call | solution.py:313
  22.0 0.6 %place.1 = (bf16[8,384]{1,0:T(8,128)(2,1)}, f32[8,128]{1,0:T(8,128)}) custom-call(bf16[8,384]{1,0:T(8,128)(2,1)S(1)} %get-tuple-element.4.refined_v, f32[8,128]{1,0:T(8,128)S(1)} %get-tuple-element.5.errors_v), custom_call_target="tpu_custom_call" | custom-call | tf_op jit(solution)/shard_map/place/pallas_call | solution.py:323

commit v2 on v1

--- a/solution.py
+++ b/solution.py
@@ -13,6 +13,12 @@
 chain_step = 65536.0
 f32 = jnp.float32
 bf16 = jnp.bfloat16
+
+
+EARLY = (2, 1, 0)
+LATE = (3,)
+TRIGGER = 0
+PIECES = (('a', (0, 1)), ('b', (2, 3)))
 
 
 def norm_rows(values):
@@ -68,6 +74,7 @@
     first = pl.multiple_of(me * rows, rows)
     step = min(count, 128)
     short = count == step
+    sub = 32
 
     hbm = (pair_h, single_h, res_h, chain_h, complex_h, pad_h, wq_h, wk_h, wv_h, wg_h, wo_h,
            wb_h, rel_h, wma_h, wmb_h, wha_h, whb_h, who_h, wp_h, pb_h)
@@ -81,25 +88,37 @@
         for i in which:
             loads[i].wait()
 
-    bits = n.bit_length() - 1
-    flips = [(1 << b) * (1 - 2 * ((me // (1 << b)) % 2)) for b in range(bits)]
-
-    def each_peer(visit):
-        if short and n == 1 << bits:
-            for s in reversed(range(1, n)):
-                visit(me + sum(flips[b] for b in range(bits) if s >> b & 1))
+    parts = 4 if n % 4 == 0 else 1
+    size = n // parts
+    mine_at = me % size
+    group = me // size
+    low = group % 2
+    groups = (group, group + 1 - 2 * low, group + 2 - 4 * (group // 2), 3 - group)[:parts]
+    span = size * rows
+
+    def each_peer(k, visit):
+        base = groups[k] * size
+
+        def body(s, _):
+            visit(base + (mine_at + s) % size)
+            return 0
+
+        if short:
+            for s in range(1 if k == 0 else 0, size):
+                body(s, 0)
         else:
-            def body(s, _):
-                visit(lax.rem(me + s, n))
-                return 0
-
-            lax.fori_loop(1, n, body, 0)
+            lax.fori_loop(1 if k == 0 else 0, size, body, 0)
+
+    def take(buf, sems, k):
+        landed = buf.at[pl.ds(0, size - (1 if k == 0 else 0))]
+        pltpu.make_async_copy(landed, landed, sems.at[k]).wait()
 
     for i in (RES, CHAIN, SINGLE):
         loads[i].start()
     barrier = pltpu.get_barrier_semaphore()
-    each_peer(lambda peer: pl.semaphore_signal(
-        barrier, inc=1, device_id={"rows": peer}, device_id_type=pl.DeviceIdType.MESH))
+    for k in reversed(range(parts)):
+        each_peer(k, lambda peer: pl.semaphore_signal(
+            barrier, inc=1, device_id={"rows": peer}, device_id_type=pl.DeviceIdType.MESH))
     for i in (REL, WB, PAIR, COMPLEX, PAD, WQ, WG, WK, WV, WO, WMB, WMA, WHA, WHB, WHO, WP, PB):
         loads[i].start()
 
@@ -142,13 +161,19 @@
 
     pl.semaphore_wait(barrier, n - 1)
 
-    def remote(src, dst, i, peer):
-        return pltpu.make_async_remote_copy(
-            src_ref=src, dst_ref=dst, send_sem=send_sem.at[i], recv_sem=recv_sem.at[i],
-            device_id={"rows": peer}, device_id_type=pl.DeviceIdType.MESH)
-
-    each_peer(lambda peer: remote(norm_s, norm_r.at[me], 0, peer).start())
-    each_peer(lambda peer: remote(bias_s.at[peer], bias_r.at[me], 1, peer).start())
+    def remote(src, dst, i, k, peer):
+        pltpu.make_async_remote_copy(
+            src_ref=src, dst_ref=dst, send_sem=send_sem.at[i], recv_sem=recv_sem.at[i, k],
+            device_id={"rows": peer}, device_id_type=pl.DeviceIdType.MESH).start()
+
+    for k in reversed(range(parts)):
+        each_peer(k, lambda peer: remote(norm_s, norm_r.at[me], 0, k, peer))
+    for k in reversed(range(parts)):
+        each_peer(k, lambda peer: remote(bias_s.at[peer], bias_r.at[me], 1, k, peer))
+
+    def send_pair(k):
+        each_peer(k, lambda peer: remote(
+            pair_v.at[pl.ds(peer * rows, rows)], pair_r.at[me], 2, k, peer))
 
     arrive(WQ)
     queries = mm(normed, wq_v[...]).astype(bf16).astype(f32)
@@ -160,10 +185,6 @@
         [jnp.where(own_head, queries[q:q + 1, :], 0.0) for q in range(rows)], axis=0).astype(bf16)
     arrive(WK)
     toward = (mm_nt(wk_v[...], q_wide) / math.sqrt(head_size)).astype(bf16)
-
-    each_peer(lambda peer: remote(
-        pair_v.at[pl.ds(peer * rows, rows)], pair_r.at[me], 2, peer).start())
-    pair_r[me] = pair_v[pl.ds(first, rows)]
 
     arrive(COMPLEX, PAD)
     lane_spot = lax.broadcasted_iota(jnp.int32, (step, spots), 1) // heads
@@ -194,13 +215,18 @@
     centers = (lax.broadcasted_iota(jnp.int32, (bins, 1), 0).astype(f32) + 0.5) * (32.0 / bins)
     arrive(WV, WO, WMB, WMA)
 
-    landed = norm_r.at[pl.ds(0, n - 1)]
-    pltpu.make_async_copy(landed, landed, recv_sem.at[0]).wait()
+    pair_r[me] = pair_v[pl.ds(first, rows)]
+
+    for k in range(parts):
+        take(norm_r, recv_sem.at[0], k)
+        if k == min(TRIGGER, parts - 1):
+            for j in EARLY:
+                send_pair(j)
     every = norm_r[...].astype(f32).reshape(count, inner).astype(bf16)
     scores = mm(every, toward)
     values = mm(every, wv_v[...]).astype(bf16)
-    landed = bias_r.at[pl.ds(0, n - 1)]
-    pltpu.make_async_copy(landed, landed, recv_sem.at[1]).wait()
+    for k in range(parts):
+        take(bias_r, recv_sem.at[1], k)
     scores = scores + bias_r[...].astype(f32).reshape(count, spots) + mask_v[...]
     expo = jnp.exp(scores - jnp.max(scores, axis=0, keepdims=True))
     weights = (expo * (1.0 / jnp.sum(expo, axis=0, keepdims=True))).astype(bf16)
@@ -216,51 +242,71 @@
     b_r[me] = factor_b
     refined_ref[...] = refined
 
-    each_peer(lambda peer: remote(b_s, b_r.at[me], 3, peer).start())
-
-    landed = pair_r.at[pl.ds(0, n - 1)]
-    pltpu.make_async_copy(landed, landed, recv_sem.at[2]).wait()
-
-    def add_block(q, _):
-        pin_v[q] = pin_v[q] + pair_r[:, q].astype(f32).reshape(count, width)
-        return 0
-
-    lax.fori_loop(0, rows, add_block, 0, unroll=short)
-
-    landed = b_r.at[pl.ds(0, n - 1)]
-    pltpu.make_async_copy(landed, landed, recv_sem.at[3]).wait()
-
-    def tail(c, _):
-        at = pl.multiple_of(c * step, step)
-        tile = pl.multiple_of(c * (step // rows), step // rows)
-        factor_b = b_r[pl.ds(tile, step // rows)].astype(f32).reshape(step, width)
-        for q in range(rows):
-            flat = pin_v[q, pl.ds(at, step), :] + a_v[q:q + 1, :] * factor_b
-            flat_v[q * step:(q + 1) * step, :] = flat
-            x_v[q * step:(q + 1) * step, :] = norm_rows(flat).astype(bf16)
+    for k in reversed(range(parts)):
+        each_peer(k, lambda peer: remote(b_s, b_r.at[me], 3, k, peer))
+    for k in LATE:
+        send_pair(k)
+
+    def tail(ks, off):
+        spans = [pl.multiple_of(groups[k] * span + off, sub) for k in ks]
+        total = len(ks) * rows * sub
+        for i, at in enumerate(spans):
+            near = pl.ds(at // rows, sub // rows)
+            factor = b_r[near].astype(f32).reshape(sub, width)
+            for q in range(rows):
+                flat = (pin_v[q, pl.ds(at, sub), :] + pair_r[near, q].astype(f32).reshape(sub, width)
+                        + a_v[q:q + 1, :] * factor)
+                row = (i * rows + q) * sub
+                flat_v[row:row + sub, :] = flat
+                x_v[row:row + sub, :] = norm_rows(flat).astype(bf16)
         cut = 256
+        tall = 128
         for k in range(0, wha_v.shape[1], cut):
             wa = wha_v[:, k:k + cut]
             wb = whb_v[:, k:k + cut]
-            for q in range(rows):
-                x = x_v[q * step:(q + 1) * step, :]
+            for r in range(0, total, tall):
+                x = x_v[r:r + tall, :]
                 half = mm(x, wa)
                 up = mm(x, wb)
-                hid_v[q * step:(q + 1) * step, k:k + cut] = (
-                    (half + half * jnp.tanh(half)) * up).astype(bf16)
-        for q in range(rows):
-            updated = flat_v[q * step:(q + 1) * step, :] + mm(hid_v[q * step:(q + 1) * step, :], who_v[...])
-            x_v[q * step:(q + 1) * step, :] = norm_rows(updated).astype(bf16)
-        found = []
-        for q in range(rows):
-            logits = mm_nt(wp_v[...], x_v[q * step:(q + 1) * step, :]) + bias_col
-            expo = jnp.exp(logits - jnp.max(logits, axis=0, keepdims=True))
-            found.append(jnp.sum(expo * centers, axis=0, keepdims=True)
+                hid_v[r:r + tall, k:k + cut] = ((half + half * jnp.tanh(half)) * up).astype(bf16)
+        for r in range(0, total, tall):
+            updated = flat_v[r:r + tall, :] + mm(hid_v[r:r + tall, :], who_v[...])
+            x_v[r:r + tall, :] = norm_rows(updated).astype(bf16)
+        per = tall // sub
+        lane_part = lax.broadcasted_iota(jnp.int32, (rows, tall), 1) // sub
+        row_part = lax.broadcasted_iota(jnp.int32, (rows, tall), 0) % per
+        row_block = lax.broadcasted_iota(jnp.int32, (rows, tall), 0) // per
+        for i, at in enumerate(spans):
+            found = jnp.zeros((rows, tall), f32)
+            for v in range(rows // per):
+                r = i * rows * sub + v * tall
+                logits = mm_nt(wp_v[...], x_v[r:r + tall, :]) + bias_col
+                expo = jnp.exp(logits - jnp.max(logits, axis=0, keepdims=True))
+                value = (jnp.sum(expo * centers, axis=0, keepdims=True)
                          / jnp.sum(expo, axis=0, keepdims=True))
-        errors_ref[:, pl.ds(at, step)] = jnp.concatenate(found, axis=0)
-        return 0
-
-    lax.fori_loop(0, count // step, tail, 0, unroll=short)
+                found = jnp.where(row_block == v, value, found)
+            spread = found
+            for u in range(1, per):
+                spread = jnp.where((lane_part + per - row_part) % per == u,
+                                   pltpu.roll(found, u * sub, 1), spread)
+            where = pl.ds(pl.multiple_of(at // tall * tall, tall), tall)
+            errors_ref[:, where] = jnp.where(
+                lane_part == (at // sub) % per, spread, errors_ref[:, where])
+
+    errors_ref[...] = jnp.zeros_like(errors_ref)
+    for name, ks in PIECES:
+        for k in ks:
+            take(pair_r, recv_sem.at[2], k)
+        for k in ks:
+            take(b_r, recv_sem.at[3], k)
+        if short:
+            tail(ks, 0)
+        else:
+            def more(c, _):
+                tail(ks, c * sub)
+                return 0
+
+            lax.fori_loop(0, span // sub, more, 0)
 
     for i, buf in enumerate((norm_r, bias_r, pair_r, b_r)):
         sent = buf.at[pl.ds(0, n - 1)]
@@ -308,7 +354,7 @@
         pltpu.VMEM((rows * step, hidden), bf16),
         pltpu.SemaphoreType.DMA((len(args),)),
         pltpu.SemaphoreType.DMA((4,)),
-        pltpu.SemaphoreType.DMA((4,)),
+        pltpu.SemaphoreType.DMA((4, 4)),
     ]
     refined, errors = pl.pallas_call(
         functools.partial(kernel, n, heads),

time: 22.8 us -> 20.7 us (0.908)
  Pallas kernels: 22 us -> 19.9 us
    pallas_call x1, Pallas kernels: 21.4 us -> 19.3 us  [on_device(): pl.pallas_call(functools.partial(kernel, n, heads), out_shape=(pltpu.VMEM...]
where the time goes in v2:
time: 20.7 us; the launch traced here: 20.6 us
  Pallas kernels  19.9 us (96%)
  between operations  0.65 us (3%)
    pallas_call x1, Pallas kernels, on_device(): pl.pallas_call(functools.partial(kernel, n, heads), out_shape=(pltpu.VMEM...  19.3 us
    pallas_call x1, Pallas kernels, on_device(): pl.pallas_call(place, out_shape=(jax.ShapeDtypeStruct((rows, inner), bf16...  0.62 us

profile of v2, /device:TPU:0, one launch (start us, length us, event | category | flops | bytes accessed | tf_op | source)
XLA Modules:
  0.0 20.6 jit_solution(8157115871529702221)
XLA Ops:
  0.6 19.3 %confidence.1 = (bf16[8,384]{1,0:T(8,128)(2,1)S(1)}, f32[8,128]{1,0:T(8,128)S(1)}) custom-call(bf16[128,8,128]{2,1,0:T(8,128)(2,1)} %pair_h.1, bf16[8,384]{1,0:T(8,128)(2,1)} %single_h.1, s32[1,128]{1,0:T(1,128)} %bitcast.9, s32[1,128]{1,0:T(1,128)} %bitcast.10, s32[1,128]{1,0:T(1,128)} %bitcast.11, s32[1,128]{1,0:T(1,128)} %bitcast.12, ...), custom_call_target="tpu_custom_call" | custom-call | tf_op jit(solution)/shard_map/confidence/pallas_call | solution.py:359
  20.0 0.6 %place.1 = (bf16[8,384]{1,0:T(8,128)(2,1)}, f32[8,128]{1,0:T(8,128)}) custom-call(bf16[8,384]{1,0:T(8,128)(2,1)S(1)} %get-tuple-element.4.refined_v, f32[8,128]{1,0:T(8,128)S(1)} %get-tuple-element.5.errors_v), custom_call_target="tpu_custom_call" | custom-call | tf_op jit(solution)/shard_map/place/pallas_call | solution.py:369

commit v3 on v2

--- a/solution.py
+++ b/solution.py
@@ -18,7 +18,7 @@
 EARLY = (2, 1, 0)
 LATE = (3,)
 TRIGGER = 0
-PIECES = (('a', (0, 1)), ('b', (2, 3)))
+PIECES = (("a", (0, 1)), ("b", (2, 3)))
 
 
 def norm_rows(values):
@@ -175,6 +175,21 @@
         each_peer(k, lambda peer: remote(
             pair_v.at[pl.ds(peer * rows, rows)], pair_r.at[me], 2, k, peer))
 
+    def send_pair_either(edge, middle):
+        inside = group * (3 - group) // 2
+        k = edge + (middle - edge) * inside
+        base = (groups[edge] + (groups[middle] - groups[edge]) * inside) * size
+        for s in range(size) if short else ():
+            peer = base + (mine_at + s) % size
+            remote(pair_v.at[pl.ds(peer * rows, rows)], pair_r.at[me], 2, k, peer)
+        if not short:
+            def body(s, _):
+                peer = base + (mine_at + s) % size
+                remote(pair_v.at[pl.ds(peer * rows, rows)], pair_r.at[me], 2, k, peer)
+                return 0
+
+            lax.fori_loop(0, size, body, 0)
+
     arrive(WQ)
     queries = mm(normed, wq_v[...]).astype(bf16).astype(f32)
     arrive(WG)
@@ -220,8 +235,9 @@
     for k in range(parts):
         take(norm_r, recv_sem.at[0], k)
         if k == min(TRIGGER, parts - 1):
-            for j in EARLY:
-                send_pair(j)
+            send_pair_either(3, 2)
+            send_pair(1)
+            send_pair(0)
     every = norm_r[...].astype(f32).reshape(count, inner).astype(bf16)
     scores = mm(every, toward)
     values = mm(every, wv_v[...]).astype(bf16)
@@ -244,8 +260,7 @@
 
     for k in reversed(range(parts)):
         each_peer(k, lambda peer: remote(b_s, b_r.at[me], 3, k, peer))
-    for k in LATE:
-        send_pair(k)
+    send_pair_either(2, 3)
 
     def tail(ks, off):
         spans = [pl.multiple_of(groups[k] * span + off, sub) for k in ks]

time: 20.7 us -> 19.8 us (0.957)
  Pallas kernels: 19.9 us -> 19 us
    pallas_call x1, Pallas kernels: 19.3 us -> 18.4 us  [on_device(): pl.pallas_call(functools.partial(kernel, n, heads), out_shape=(pltpu.VMEM...]
where the time goes in v3:
time: 19.8 us; the launch traced here: 19.6 us
  Pallas kernels  19 us (96%)
  between operations  0.65 us (3%)
    pallas_call x1, Pallas kernels, on_device(): pl.pallas_call(functools.partial(kernel, n, heads), out_shape=(pltpu.VMEM...  18.4 us
    pallas_call x1, Pallas kernels, on_device(): pl.pallas_call(place, out_shape=(jax.ShapeDtypeStruct((rows, inner), bf16...  0.62 us

profile of v3, /device:TPU:0, one launch (start us, length us, event | category | flops | bytes accessed | tf_op | source)
XLA Modules:
  0.0 19.6 jit_solution(16307773516228134575)
XLA Ops:
  0.6 18.4 %confidence.1 = (bf16[8,384]{1,0:T(8,128)(2,1)S(1)}, f32[8,128]{1,0:T(8,128)S(1)}) custom-call(bf16[128,8,128]{2,1,0:T(8,128)(2,1)} %pair_h.1, bf16[8,384]{1,0:T(8,128)(2,1)} %single_h.1, s32[1,128]{1,0:T(1,128)} %bitcast.9, s32[1,128]{1,0:T(1,128)} %bitcast.10, s32[1,128]{1,0:T(1,128)} %bitcast.11, s32[1,128]{1,0:T(1,128)} %bitcast.12, ...), custom_call_target="tpu_custom_call" | custom-call | tf_op jit(solution)/shard_map/confidence/pallas_call | solution.py:374
  19.0 0.6 %place.1 = (bf16[8,384]{1,0:T(8,128)(2,1)}, f32[8,128]{1,0:T(8,128)}) custom-call(bf16[8,384]{1,0:T(8,128)(2,1)S(1)} %get-tuple-element.4.refined_v, f32[8,128]{1,0:T(8,128)S(1)} %get-tuple-element.5.errors_v), custom_call_target="tpu_custom_call" | custom-call | tf_op jit(solution)/shard_map/place/pallas_call | solution.py:384

commit v4 on v3

--- a/solution.py
+++ b/solution.py
@@ -15,10 +15,7 @@
 bf16 = jnp.bfloat16
 
 
-EARLY = (2, 1, 0)
-LATE = (3,)
 TRIGGER = 0
-PIECES = (("a", (0, 1)), ("b", (2, 3)))
 
 
 def norm_rows(values):
@@ -62,7 +59,7 @@
     pair_v, single_v, res_v, chain_v, complex_v, pad_v,
     wq_v, wk_v, wv_v, wg_v, wo_v, wb_v, rel_v, wma_v, wmb_v, wha_v, whb_v, who_v, wp_v, pb_v,
     code_v, ccol_v, mask_v, bias_s, bias_r, norm_s, norm_r, pair_r, b_s, b_r, a_v, pin_v,
-    flat_v, x_v, hid_v,
+    flat_v, x_v, hid_v, wab_v,
     local_sem, send_sem, recv_sem,
 ):
     me = lax.axis_index("rows")
@@ -131,7 +128,7 @@
     mine = single_v[...].astype(f32)
     normed = norm_rows(mine).astype(bf16)
     norm_s[...] = normed
-    norm_r[me] = normed
+    norm_r[me // 2, me % 2] = normed
 
     arrive(REL, WB, PAIR)
     rel = rel_v[...]
@@ -166,8 +163,29 @@
             src_ref=src, dst_ref=dst, send_sem=send_sem.at[i], recv_sem=recv_sem.at[i, k],
             device_id={"rows": peer}, device_id_type=pl.DeviceIdType.MESH).start()
 
+    side = me % 2
+    partner = me + 1 - 2 * side
+    pairs = size // 2
+
+    def spread_single(k):
+        base = groups[k] * size
+
+        def body(s, _):
+            chip = base + 2 * ((mine_at // 2 + s) % pairs)
+            for core in (0, 1) if k == 0 else (side,):
+                remote(norm_s, norm_r.at[me // 2, side], 0, k, chip + core)
+            return 0
+
+        if short:
+            for s in range(1 if k == 0 else 0, pairs):
+                body(s, 0)
+        else:
+            lax.fori_loop(1 if k == 0 else 0, pairs, body, 0)
+        if k == 0:
+            remote(norm_s, norm_r.at[me // 2, side], 5, 0, partner)
+
     for k in reversed(range(parts)):
-        each_peer(k, lambda peer: remote(norm_s, norm_r.at[me], 0, k, peer))
+        spread_single(k)
     for k in reversed(range(parts)):
         each_peer(k, lambda peer: remote(bias_s.at[peer], bias_r.at[me], 1, k, peer))
 
@@ -229,15 +247,31 @@
     bias_col = column(pb_v[...])
     centers = (lax.broadcasted_iota(jnp.int32, (bins, 1), 0).astype(f32) + 0.5) * (32.0 / bins)
     arrive(WV, WO, WMB, WMA)
+    wab_v[:, :width] = wmb_v[...]
+    wab_v[:, width:] = wma_v[...]
+    wab_sum = mm(jnp.ones((rows, inner), bf16), wab_v[...])
 
     pair_r[me] = pair_v[pl.ds(first, rows)]
 
+    def take_single(k):
+        if k == 0:
+            if pairs > 1:
+                landed = norm_r.at[pl.ds(0, pairs - 1)]
+                pltpu.make_async_copy(landed, landed, recv_sem.at[0, 0]).wait()
+            pltpu.make_async_copy(norm_s, norm_s, recv_sem.at[5, 0]).wait()
+        else:
+            half = norm_r.at[pl.ds(groups[k] * pairs, pairs), side]
+            pltpu.make_async_copy(half, half, recv_sem.at[0, k]).wait()
+            remote(half, half, 4, k, partner)
+
+    send_pair_either(3, 2)
+    send_pair(1)
+    send_pair(0)
     for k in range(parts):
-        take(norm_r, recv_sem.at[0], k)
-        if k == min(TRIGGER, parts - 1):
-            send_pair_either(3, 2)
-            send_pair(1)
-            send_pair(0)
+        take_single(k)
+    for k in range(1, parts):
+        half = norm_r.at[pl.ds(0, pairs), 0]
+        pltpu.make_async_copy(half, half, recv_sem.at[4, k]).wait()
     every = norm_r[...].astype(f32).reshape(count, inner).astype(bf16)
     scores = mm(every, toward)
     values = mm(every, wv_v[...]).astype(bf16)
@@ -251,10 +285,15 @@
         [jnp.sum(jnp.where(own_head, mixed_heads[q * heads:(q + 1) * heads, :], 0.0),
                  axis=0, keepdims=True) for q in range(rows)], axis=0)
     refined = (mine + mm((gating * attended).astype(bf16), wo_v[...])).astype(bf16)
-    renormed = norm_rows(refined.astype(f32)).astype(bf16)
-    factor_b = mm(renormed, wmb_v[...]).astype(bf16)
+    raw = mm(refined, wab_v[...])
+    exact = refined.astype(f32)
+    middle = jnp.mean(exact, axis=-1, keepdims=True)
+    away = exact - middle
+    scale = lax.rsqrt(jnp.mean(away * away, axis=-1, keepdims=True) + epsilon)
+    factors = ((raw - middle * wab_sum) * scale).astype(bf16)
+    factor_b = factors[:, :width]
     b_s[...] = factor_b
-    a_v[...] = mm(renormed, wma_v[...]).astype(bf16).astype(f32)
+    a_v[...] = factors[:, width:].astype(f32)
     b_r[me] = factor_b
     refined_ref[...] = refined
 
@@ -262,70 +301,117 @@
         each_peer(k, lambda peer: remote(b_s, b_r.at[me], 3, k, peer))
     send_pair_either(2, 3)
 
-    def tail(ks, off):
-        spans = [pl.multiple_of(groups[k] * span + off, sub) for k in ks]
-        total = len(ks) * rows * sub
-        for i, at in enumerate(spans):
-            near = pl.ds(at // rows, sub // rows)
-            factor = b_r[near].astype(f32).reshape(sub, width)
-            for q in range(rows):
-                flat = (pin_v[q, pl.ds(at, sub), :] + pair_r[near, q].astype(f32).reshape(sub, width)
-                        + a_v[q:q + 1, :] * factor)
-                row = (i * rows + q) * sub
-                flat_v[row:row + sub, :] = flat
-                x_v[row:row + sub, :] = norm_rows(flat).astype(bf16)
+    per = step // sub
+    lane_part = lax.broadcasted_iota(jnp.int32, (rows, step), 1) // sub
+    row_part = lax.broadcasted_iota(jnp.int32, (rows, step), 0) % per
+    row_block = lax.broadcasted_iota(jnp.int32, (rows, step), 0) // per
+    block = rows * sub
+
+    def place_of(k, off):
+        return pl.multiple_of(groups[k] * span + off, sub)
+
+    def mix(k, off):
+        at = place_of(k, off)
+        near = pl.ds(at // rows, sub // rows)
+        factor = b_r[near].astype(f32).reshape(sub, width)
+        for q in range(rows):
+            flat = (pin_v[q, pl.ds(at, sub), :] + pair_r[near, q].astype(f32).reshape(sub, width)
+                    + a_v[q:q + 1, :] * factor)
+            row = k * block + q * sub
+            flat_v[row:row + sub, :] = flat
+            x_v[row:row + sub, :] = norm_rows(flat).astype(bf16)
+
+    def expand(ks):
         cut = 256
-        tall = 128
-        for k in range(0, wha_v.shape[1], cut):
-            wa = wha_v[:, k:k + cut]
-            wb = whb_v[:, k:k + cut]
-            for r in range(0, total, tall):
-                x = x_v[r:r + tall, :]
-                half = mm(x, wa)
-                up = mm(x, wb)
-                hid_v[r:r + tall, k:k + cut] = ((half + half * jnp.tanh(half)) * up).astype(bf16)
-        for r in range(0, total, tall):
-            updated = flat_v[r:r + tall, :] + mm(hid_v[r:r + tall, :], who_v[...])
-            x_v[r:r + tall, :] = norm_rows(updated).astype(bf16)
-        per = tall // sub
-        lane_part = lax.broadcasted_iota(jnp.int32, (rows, tall), 1) // sub
-        row_part = lax.broadcasted_iota(jnp.int32, (rows, tall), 0) % per
-        row_block = lax.broadcasted_iota(jnp.int32, (rows, tall), 0) // per
-        for i, at in enumerate(spans):
-            found = jnp.zeros((rows, tall), f32)
-            for v in range(rows // per):
-                r = i * rows * sub + v * tall
-                logits = mm_nt(wp_v[...], x_v[r:r + tall, :]) + bias_col
-                expo = jnp.exp(logits - jnp.max(logits, axis=0, keepdims=True))
-                value = (jnp.sum(expo * centers, axis=0, keepdims=True)
-                         / jnp.sum(expo, axis=0, keepdims=True))
-                found = jnp.where(row_block == v, value, found)
-            spread = found
-            for u in range(1, per):
-                spread = jnp.where((lane_part + per - row_part) % per == u,
-                                   pltpu.roll(found, u * sub, 1), spread)
-            where = pl.ds(pl.multiple_of(at // tall * tall, tall), tall)
-            errors_ref[:, where] = jnp.where(
-                lane_part == (at // sub) % per, spread, errors_ref[:, where])
+        for c in range(0, wha_v.shape[1], cut):
+            wa = wha_v[:, c:c + cut]
+            wb = whb_v[:, c:c + cut]
+            for k in ks:
+                for r in range(k * block, (k + 1) * block, step):
+                    x = x_v[r:r + step, :]
+                    half = mm(x, wa)
+                    up = mm(x, wb)
+                    hid_v[r:r + step, c:c + cut] = ((half + half * jnp.tanh(half)) * up).astype(bf16)
+
+    def reduce(k):
+        for r in range(k * block, (k + 1) * block, step):
+            updated = flat_v[r:r + step, :] + mm(hid_v[r:r + step, :], who_v[...])
+            x_v[r:r + step, :] = norm_rows(updated).astype(bf16)
+
+    def grade(k, off):
+        found = jnp.zeros((rows, step), f32)
+        for v in range(rows // per):
+            r = k * block + v * step
+            logits = mm_nt(wp_v[...], x_v[r:r + step, :]) + bias_col
+            expo = jnp.exp(logits - jnp.max(logits, axis=0, keepdims=True))
+            value = (jnp.sum(expo * centers, axis=0, keepdims=True)
+                     / jnp.sum(expo, axis=0, keepdims=True))
+            found = jnp.where(row_block == v, value, found)
+        spread = found
+        for u in range(1, per):
+            spread = jnp.where((lane_part + per - row_part) % per == u,
+                               pltpu.roll(found, u * sub, 1), spread)
+        at = place_of(k, off)
+        where = pl.ds(pl.multiple_of(at // step * step, step), step)
+        errors_ref[:, where] = jnp.where(
+            lane_part == (at // sub) % per, spread, errors_ref[:, where])
+
+    def ready(k):
+        take(pair_r, recv_sem.at[2], k)
+        take(b_r, recv_sem.at[3], k)
 
     errors_ref[...] = jnp.zeros_like(errors_ref)
-    for name, ks in PIECES:
-        for k in ks:
-            take(pair_r, recv_sem.at[2], k)
-        for k in ks:
-            take(b_r, recv_sem.at[3], k)
-        if short:
-            tail(ks, 0)
-        else:
-            def more(c, _):
-                tail(ks, c * sub)
-                return 0
-
-            lax.fori_loop(0, span // sub, more, 0)
-
-    for i, buf in enumerate((norm_r, bias_r, pair_r, b_r)):
-        sent = buf.at[pl.ds(0, n - 1)]
-        pltpu.make_async_copy(sent, sent, send_sem.at[i]).wait()
+    if short and parts == 4:
+        take(b_r, recv_sem.at[3], 0)
+        take(pair_r, recv_sem.at[2], 0)
+        take(b_r, recv_sem.at[3], 1)
+        take(pair_r, recv_sem.at[2], 1)
+        mix(0, 0)
+        mix(1, 0)
+        expand((0,))
+        expand((1,))
+        reduce(0)
+        reduce(1)
+        take(b_r, recv_sem.at[3], 2)
+        take(pair_r, recv_sem.at[2], 2)
+        take(b_r, recv_sem.at[3], 3)
+        take(pair_r, recv_sem.at[2], 3)
+        mix(2, 0)
+        grade(0, 0)
+        mix(3, 0)
+        expand((2,))
+        grade(1, 0)
+        expand((3,))
+        reduce(2)
+        reduce(3)
+        grade(2, 0)
+        grade(3, 0)
+    else:
+        for k in range(parts):
+            ready(k)
+
+        def more(c, _):
+            for k in range(parts):
+                mix(k, c * sub)
+                expand((k,))
+                reduce(k)
+                grade(k, c * sub)
+            return 0
+
+        lax.fori_loop(0, span // sub, more, 0)
+
+    def sent(buf, i, amount):
+        out = buf.at[pl.ds(0, amount)]
+        pltpu.make_async_copy(out, out, send_sem.at[i]).wait()
+
+    sent(bias_r, 1, n - 1)
+    sent(pair_r, 2, n - 1)
+    sent(b_r, 3, n - 1)
+    pltpu.make_async_copy(norm_s, norm_s, send_sem.at[5]).wait()
+    if n > 2:
+        sent(norm_r, 0, (size - 2 + (parts - 1) * pairs) // 2)
+    if parts > 1:
+        sent(norm_r, 4, (parts - 1) * pairs // 2)
 
 
 def place(refined_v, errors_v, refined_h, errors_h, sem):
@@ -358,7 +444,7 @@
         pltpu.VMEM((n, rows, spots), bf16),
         pltpu.VMEM((n, rows, spots), bf16),
         pltpu.VMEM((rows, inner), bf16),
-        pltpu.VMEM((n, rows, inner), bf16),
+        pltpu.VMEM((n // 2, 2, rows, inner), bf16),
         pltpu.VMEM((n, rows, rows, width), bf16),
         pltpu.VMEM((rows, width), bf16),
         pltpu.VMEM((n, rows, width), bf16),
@@ -367,9 +453,10 @@
         pltpu.VMEM((rows * step, width), f32),
         pltpu.VMEM((rows * step, width), bf16),
         pltpu.VMEM((rows * step, hidden), bf16),
+        pltpu.VMEM((inner, 2 * width), bf16),
         pltpu.SemaphoreType.DMA((len(args),)),
-        pltpu.SemaphoreType.DMA((4,)),
-        pltpu.SemaphoreType.DMA((4, 4)),
+        pltpu.SemaphoreType.DMA((6,)),
+        pltpu.SemaphoreType.DMA((6, 4)),
     ]
     refined, errors = pl.pallas_call(
         functools.partial(kernel, n, heads),

time: 19.8 us -> 19 us (0.960)
  Pallas kernels: 19 us -> 18.2 us
    pallas_call x1, Pallas kernels: 18.4 us -> 17.6 us  [on_device(): pl.pallas_call(functools.partial(kernel, n, heads), out_shape=(pltpu.VMEM...]
where the time goes in v4:
time: 19 us; the launch traced here: 18.8 us
  Pallas kernels  18.2 us (96%)
  between operations  0.65 us (3%)
    pallas_call x1, Pallas kernels, on_device(): pl.pallas_call(functools.partial(kernel, n, heads), out_shape=(pltpu.VMEM...  17.6 us
    pallas_call x1, Pallas kernels, on_device(): pl.pallas_call(place, out_shape=(jax.ShapeDtypeStruct((rows, inner), bf16...  0.62 us

profile of v4, /device:TPU:0, one launch (start us, length us, event | category | flops | bytes accessed | tf_op | source)
XLA Modules:
  0.0 18.8 jit_solution(1075601386895169535)
XLA Ops:
  0.6 17.6 %confidence.1 = (bf16[8,384]{1,0:T(8,128)(2,1)S(1)}, f32[8,128]{1,0:T(8,128)S(1)}) custom-call(bf16[128,8,128]{2,1,0:T(8,128)(2,1)} %pair_h.1, bf16[8,384]{1,0:T(8,128)(2,1)} %single_h.1, s32[1,128]{1,0:T(1,128)} %bitcast.9, s32[1,128]{1,0:T(1,128)} %bitcast.10, s32[1,128]{1,0:T(1,128)} %bitcast.11, s32[1,128]{1,0:T(1,128)} %bitcast.12, ...), custom_call_target="tpu_custom_call" | custom-call | tf_op jit(solution)/shard_map/confidence/pallas_call | solution.py:461
  18.2 0.6 %place.1 = (bf16[8,384]{1,0:T(8,128)(2,1)}, f32[8,128]{1,0:T(8,128)}) custom-call(bf16[8,384]{1,0:T(8,128)(2,1)S(1)} %get-tuple-element.4.refined_v, f32[8,128]{1,0:T(8,128)S(1)} %get-tuple-element.5.errors_v), custom_call_target="tpu_custom_call" | custom-call | tf_op jit(solution)/shard_map/place/pallas_call | solution.py:471

commit v5 on v4

--- a/solution.py
+++ b/solution.py
@@ -13,9 +13,6 @@
 chain_step = 65536.0
 f32 = jnp.float32
 bf16 = jnp.bfloat16
-
-
-TRIGGER = 0
 
 
 def norm_rows(values):
@@ -59,7 +56,7 @@
     pair_v, single_v, res_v, chain_v, complex_v, pad_v,
     wq_v, wk_v, wv_v, wg_v, wo_v, wb_v, rel_v, wma_v, wmb_v, wha_v, whb_v, who_v, wp_v, pb_v,
     code_v, ccol_v, mask_v, bias_s, bias_r, norm_s, norm_r, pair_r, b_s, b_r, a_v, pin_v,
-    flat_v, x_v, hid_v, wab_v,
+    flat_v, x_v, hid_v, wab_v, scale_v, square_v,
     local_sem, send_sem, recv_sem,
 ):
     me = lax.axis_index("rows")
@@ -126,6 +123,7 @@
 
     arrive(SINGLE)
     mine = single_v[...].astype(f32)
+    center = jnp.mean(mine, axis=-1, keepdims=True)
     normed = norm_rows(mine).astype(bf16)
     norm_s[...] = normed
     norm_r[me // 2, me % 2] = normed
@@ -243,8 +241,11 @@
 
     arrive(WHA, WHB, WHO, WP, PB)
     wha_v[...] = (wha_v[...].astype(f32) * 0.5).astype(bf16)
+    down = who_v[...].astype(f32)
+    who_v[...] = (down - jnp.mean(down, axis=-1, keepdims=True)).astype(bf16)
     bins = wp_v.shape[0]
     bias_col = column(pb_v[...])
+    even = jnp.full((8, width), 1.0 / width, bf16)
     centers = (lax.broadcasted_iota(jnp.int32, (bins, 1), 0).astype(f32) + 0.5) * (32.0 / bins)
     arrive(WV, WO, WMB, WMA)
     wab_v[:, :width] = wmb_v[...]
@@ -287,9 +288,11 @@
     refined = (mine + mm((gating * attended).astype(bf16), wo_v[...])).astype(bf16)
     raw = mm(refined, wab_v[...])
     exact = refined.astype(f32)
-    middle = jnp.mean(exact, axis=-1, keepdims=True)
-    away = exact - middle
-    scale = lax.rsqrt(jnp.mean(away * away, axis=-1, keepdims=True) + epsilon)
+    away = exact - center
+    shift = jnp.mean(away, axis=-1, keepdims=True)
+    spread = jnp.maximum(jnp.mean(away * away, axis=-1, keepdims=True) - shift * shift, 0.0)
+    middle = center + shift
+    scale = lax.rsqrt(spread + epsilon)
     factors = ((raw - middle * wab_sum) * scale).astype(bf16)
     factor_b = factors[:, :width]
     b_s[...] = factor_b
@@ -318,8 +321,11 @@
             flat = (pin_v[q, pl.ds(at, sub), :] + pair_r[near, q].astype(f32).reshape(sub, width)
                     + a_v[q:q + 1, :] * factor)
             row = k * block + q * sub
-            flat_v[row:row + sub, :] = flat
-            x_v[row:row + sub, :] = norm_rows(flat).astype(bf16)
+            center = flat - jnp.mean(flat, axis=-1, keepdims=True)
+            spread = jnp.mean(center * center, axis=-1, keepdims=True)
+            flat_v[row:row + sub, :] = center
+            x_v[row:row + sub, :] = center.astype(bf16)
+            scale_v[row:row + sub, :] = jnp.broadcast_to(lax.rsqrt(spread + epsilon), (sub, 128))
 
     def expand(ks):
         cut = 256
@@ -329,20 +335,23 @@
             for k in ks:
                 for r in range(k * block, (k + 1) * block, step):
                     x = x_v[r:r + step, :]
-                    half = mm(x, wa)
-                    up = mm(x, wb)
+                    scale = jnp.tile(scale_v[r:r + step, :], (1, cut // 128))
+                    half = mm(x, wa) * scale
+                    up = mm(x, wb) * scale
                     hid_v[r:r + step, c:c + cut] = ((half + half * jnp.tanh(half)) * up).astype(bf16)
 
     def reduce(k):
         for r in range(k * block, (k + 1) * block, step):
-            updated = flat_v[r:r + step, :] + mm(hid_v[r:r + step, :], who_v[...])
-            x_v[r:r + step, :] = norm_rows(updated).astype(bf16)
+            center = flat_v[r:r + step, :] + mm(hid_v[r:r + step, :], who_v[...])
+            x_v[r:r + step, :] = center.astype(bf16)
+            square_v[r:r + step, :] = (center * center).astype(bf16)
 
     def grade(k, off):
         found = jnp.zeros((rows, step), f32)
         for v in range(rows // per):
             r = k * block + v * step
-            logits = mm_nt(wp_v[...], x_v[r:r + step, :]) + bias_col
+            spread = mm_nt(even, square_v[r:r + step, :])[0:1]
+            logits = mm_nt(wp_v[...], x_v[r:r + step, :]) * lax.rsqrt(spread + epsilon) + bias_col
             expo = jnp.exp(logits - jnp.max(logits, axis=0, keepdims=True))
             value = (jnp.sum(expo * centers, axis=0, keepdims=True)
                      / jnp.sum(expo, axis=0, keepdims=True))
@@ -368,23 +377,22 @@
         take(pair_r, recv_sem.at[2], 1)
         mix(0, 0)
         mix(1, 0)
-        expand((0,))
-        expand((1,))
+        expand((0,1,))
         reduce(0)
         reduce(1)
         take(b_r, recv_sem.at[3], 2)
         take(pair_r, recv_sem.at[2], 2)
+        mix(2, 0)
+        grade(0, 0)
+        grade(1, 0)
+        expand((2,))
         take(b_r, recv_sem.at[3], 3)
         take(pair_r, recv_sem.at[2], 3)
-        mix(2, 0)
-        grade(0, 0)
         mix(3, 0)
-        expand((2,))
-        grade(1, 0)
+        reduce(2)
         expand((3,))
-        reduce(2)
+        grade(2, 0)
         reduce(3)
-        grade(2, 0)
         grade(3, 0)
     else:
         for k in range(parts):
@@ -454,6 +462,8 @@
         pltpu.VMEM((rows * step, width), bf16),
         pltpu.VMEM((rows * step, hidden), bf16),
         pltpu.VMEM((inner, 2 * width), bf16),
+        pltpu.VMEM((rows * step, 128), f32),
+        pltpu.VMEM((rows * step, width), bf16),
         pltpu.SemaphoreType.DMA((len(args),)),
         pltpu.SemaphoreType.DMA((6,)),
         pltpu.SemaphoreType.DMA((6, 4)),

time: 19 us -> 18.4 us (0.968)
  Pallas kernels: 18.2 us -> 17.6 us
    pallas_call x1, Pallas kernels: 17.6 us -> 17 us  [on_device(): pl.pallas_call(functools.partial(kernel, n, heads), out_shape=(pltpu.VMEM...]
where the time goes in v5:
time: 18.4 us; the launch traced here: 18.3 us
  Pallas kernels  17.6 us (96%)
  between operations  0.65 us (4%)
    pallas_call x1, Pallas kernels, on_device(): pl.pallas_call(functools.partial(kernel, n, heads), out_shape=(pltpu.VMEM...  17 us
    pallas_call x1, Pallas kernels, on_device(): pl.pallas_call(place, out_shape=(jax.ShapeDtypeStruct((rows, inner), bf16...  0.62 us

profile of v5, /device:TPU:0, one launch (start us, length us, event | category | flops | bytes accessed | tf_op | source)
XLA Modules:
  0.0 18.3 jit_solution(13427806541252674422)
XLA Ops:
  0.6 17.0 %confidence.1 = (bf16[8,384]{1,0:T(8,128)(2,1)S(1)}, f32[8,128]{1,0:T(8,128)S(1)}) custom-call(bf16[128,8,128]{2,1,0:T(8,128)(2,1)} %pair_h.1, bf16[8,384]{1,0:T(8,128)(2,1)} %single_h.1, s32[1,128]{1,0:T(1,128)} %bitcast.9, s32[1,128]{1,0:T(1,128)} %bitcast.10, s32[1,128]{1,0:T(1,128)} %bitcast.11, s32[1,128]{1,0:T(1,128)} %bitcast.12, ...), custom_call_target="tpu_custom_call" | custom-call | tf_op jit(solution)/shard_map/confidence/pallas_call | solution.py:471
  17.7 0.6 %place.1 = (bf16[8,384]{1,0:T(8,128)(2,1)}, f32[8,128]{1,0:T(8,128)}) custom-call(bf16[8,384]{1,0:T(8,128)(2,1)S(1)} %get-tuple-element.4.refined_v, f32[8,128]{1,0:T(8,128)S(1)} %get-tuple-element.5.errors_v), custom_call_target="tpu_custom_call" | custom-call | tf_op jit(solution)/shard_map/place/pallas_call | solution.py:481

commit v6 on v5

--- a/solution.py
+++ b/solution.py
@@ -56,7 +56,7 @@
     pair_v, single_v, res_v, chain_v, complex_v, pad_v,
     wq_v, wk_v, wv_v, wg_v, wo_v, wb_v, rel_v, wma_v, wmb_v, wha_v, whb_v, who_v, wp_v, pb_v,
     code_v, ccol_v, mask_v, bias_s, bias_r, norm_s, norm_r, pair_r, b_s, b_r, a_v, pin_v,
-    flat_v, x_v, hid_v, wab_v, scale_v, square_v,
+    flat_v, x_v, hid_v, wab_v, scale_v, square_v, score_v,
     local_sem, send_sem, recv_sem,
 ):
     me = lax.axis_index("rows")
@@ -107,13 +107,11 @@
         landed = buf.at[pl.ds(0, size - (1 if k == 0 else 0))]
         pltpu.make_async_copy(landed, landed, sems.at[k]).wait()
 
-    for i in (RES, CHAIN, SINGLE):
-        loads[i].start()
     barrier = pltpu.get_barrier_semaphore()
     for k in reversed(range(parts)):
         each_peer(k, lambda peer: pl.semaphore_signal(
             barrier, inc=1, device_id={"rows": peer}, device_id_type=pl.DeviceIdType.MESH))
-    for i in (REL, WB, PAIR, COMPLEX, PAD, WQ, WG, WK, WV, WO, WMB, WMA, WHA, WHB, WHO, WP, PB):
+    for i in (RES, CHAIN, SINGLE, REL, WB, PAIR, COMPLEX, PAD, WQ, WG, WK, WV, WO, WMB, WMA, WHA, WHB, WHO, WP, PB):
         loads[i].start()
 
     arrive(RES, CHAIN)
@@ -131,7 +129,7 @@
     arrive(REL, WB, PAIR)
     rel = rel_v[...]
     tile_h = jnp.where(
-        lax.broadcasted_iota(jnp.int32, (heads, spots), 1) % heads
+        lax.broadcasted_iota(jnp.int32, (heads, spots), 1) // rows
         == lax.broadcasted_iota(jnp.int32, (heads, spots), 0), 1.0, 0.0).astype(bf16)
     w_tiled = mm_tn(wb_v[...], tile_h).astype(bf16)
     code_keys = code_v[pl.ds(first, rows), :classes]
@@ -144,7 +142,7 @@
         cells = mm(hot, rel) + pair_v[pl.ds(at, step)].astype(f32).reshape(step * rows, width)
         out = mm(norm_rows(cells).astype(bf16), w_tiled)
         out = out.reshape(step // rows, rows, rows, spots)
-        lane_q = lax.broadcasted_iota(jnp.int32, (1, 1, spots), 2) // heads
+        lane_q = lax.broadcasted_iota(jnp.int32, (1, 1, spots), 2) % rows
         total = jnp.where(lane_q == 0, out[:, 0], 0.0)
         for q in range(1, rows):
             total = jnp.where(lane_q == q, out[:, q], total)
@@ -191,39 +189,39 @@
         each_peer(k, lambda peer: remote(
             pair_v.at[pl.ds(peer * rows, rows)], pair_r.at[me], 2, k, peer))
 
-    def send_pair_either(edge, middle):
+    def send_pair_either(edge, middle, low, high):
         inside = group * (3 - group) // 2
         k = edge + (middle - edge) * inside
         base = (groups[edge] + (groups[middle] - groups[edge]) * inside) * size
-        for s in range(size) if short else ():
+
+        def body(s, _):
             peer = base + (mine_at + s) % size
             remote(pair_v.at[pl.ds(peer * rows, rows)], pair_r.at[me], 2, k, peer)
-        if not short:
-            def body(s, _):
-                peer = base + (mine_at + s) % size
-                remote(pair_v.at[pl.ds(peer * rows, rows)], pair_r.at[me], 2, k, peer)
-                return 0
-
-            lax.fori_loop(0, size, body, 0)
+            return 0
+
+        if short:
+            for s in range(low, high):
+                body(s, 0)
+        else:
+            lax.fori_loop(low, high, body, 0)
 
     arrive(WQ)
     queries = mm(normed, wq_v[...]).astype(bf16).astype(f32)
     arrive(WG)
     gating = jax.nn.sigmoid(mm(normed, wg_v[...]))
-    head_of = lax.broadcasted_iota(jnp.int32, (heads, inner), 1) // head_size
-    own_head = head_of == lax.broadcasted_iota(jnp.int32, (heads, inner), 0)
+    head_of = lax.broadcasted_iota(jnp.int32, (rows, inner), 1) // head_size
     q_wide = jnp.concatenate(
-        [jnp.where(own_head, queries[q:q + 1, :], 0.0) for q in range(rows)], axis=0).astype(bf16)
+        [jnp.where(head_of == h, queries, 0.0) for h in range(heads)], axis=0).astype(bf16)
     arrive(WK)
     toward = (mm_nt(wk_v[...], q_wide) / math.sqrt(head_size)).astype(bf16)
 
     arrive(COMPLEX, PAD)
-    lane_spot = lax.broadcasted_iota(jnp.int32, (step, spots), 1) // heads
+    lane_spot = lax.broadcasted_iota(jnp.int32, (step, spots), 1) % rows
     for k in range(0, count, step):
         ccol_v[k:k + step, :] = jnp.broadcast_to(
             column(complex_v[:, k:k + step].astype(f32)), (step, 128))
     mine_c = ccol_v[pl.ds(first, rows), 0:1]
-    lane_row = lax.broadcasted_iota(jnp.int32, (rows, spots), 1) // heads
+    lane_row = lax.broadcasted_iota(jnp.int32, (rows, spots), 1) % rows
     pick = lane_row == lax.broadcasted_iota(jnp.int32, (rows, spots), 0)
     query_c = jnp.sum(jnp.where(pick, mine_c, 0.0), axis=0, keepdims=True)
     for k in range(0, count, step):
@@ -265,26 +263,27 @@
             pltpu.make_async_copy(half, half, recv_sem.at[0, k]).wait()
             remote(half, half, 4, k, partner)
 
-    send_pair_either(3, 2)
+    send_pair_either(3, 2, 0, size)
     send_pair(1)
     send_pair(0)
+    send_pair_either(2, 3, 0, size * 2 // 4)
     for k in range(parts):
         take_single(k)
     for k in range(1, parts):
         half = norm_r.at[pl.ds(0, pairs), 0]
         pltpu.make_async_copy(half, half, recv_sem.at[4, k]).wait()
     every = norm_r[...].astype(f32).reshape(count, inner).astype(bf16)
-    scores = mm(every, toward)
-    values = mm(every, wv_v[...]).astype(bf16)
+    score_v[...] = mm(every, toward) + mask_v[...]
     for k in range(parts):
         take(bias_r, recv_sem.at[1], k)
-    scores = scores + bias_r[...].astype(f32).reshape(count, spots) + mask_v[...]
+    values = mm(every, wv_v[...]).astype(bf16)
+    scores = score_v[...] + bias_r[...].astype(f32).reshape(count, spots)
     expo = jnp.exp(scores - jnp.max(scores, axis=0, keepdims=True))
     weights = (expo * (1.0 / jnp.sum(expo, axis=0, keepdims=True))).astype(bf16)
     mixed_heads = mm_tn(weights, values)
-    attended = jnp.concatenate(
-        [jnp.sum(jnp.where(own_head, mixed_heads[q * heads:(q + 1) * heads, :], 0.0),
-                 axis=0, keepdims=True) for q in range(rows)], axis=0)
+    attended = mixed_heads[:rows, :]
+    for h in range(1, heads):
+        attended = jnp.where(head_of == h, mixed_heads[h * rows:(h + 1) * rows, :], attended)
     refined = (mine + mm((gating * attended).astype(bf16), wo_v[...])).astype(bf16)
     raw = mm(refined, wab_v[...])
     exact = refined.astype(f32)
@@ -302,7 +301,7 @@
 
     for k in reversed(range(parts)):
         each_peer(k, lambda peer: remote(b_s, b_r.at[me], 3, k, peer))
-    send_pair_either(2, 3)
+    send_pair_either(2, 3, size * 2 // 4, size)
 
     per = step // sub
     lane_part = lax.broadcasted_iota(jnp.int32, (rows, step), 1) // sub
@@ -464,6 +463,7 @@
         pltpu.VMEM((inner, 2 * width), bf16),
         pltpu.VMEM((rows * step, 128), f32),
         pltpu.VMEM((rows * step, width), bf16),
+        pltpu.VMEM((count, spots), f32),
         pltpu.SemaphoreType.DMA((len(args),)),
         pltpu.SemaphoreType.DMA((6,)),
         pltpu.SemaphoreType.DMA((6, 4)),

time: 18.4 us -> 18.3 us (level)
  no operation moved by 1% of the time
where the time goes in v6:
time: 18.3 us; the launch traced here: 18.2 us
  Pallas kernels  17.5 us (96%)
  between operations  0.65 us (4%)
    pallas_call x1, Pallas kernels, on_device(): pl.pallas_call(functools.partial(kernel, n, heads), out_shape=(pltpu.VMEM...  16.9 us
    pallas_call x1, Pallas kernels, on_device(): pl.pallas_call(place, out_shape=(jax.ShapeDtypeStruct((rows, inner), bf16...  0.62 us

profile of v6, /device:TPU:0, one launch (start us, length us, event | category | flops | bytes accessed | tf_op | source)
XLA Modules:
  0.0 18.2 jit_solution(17453104579678648746)
XLA Ops:
  0.6 16.9 %confidence.1 = (bf16[8,384]{1,0:T(8,128)(2,1)S(1)}, f32[8,128]{1,0:T(8,128)S(1)}) custom-call(bf16[128,8,128]{2,1,0:T(8,128)(2,1)} %pair_h.1, bf16[8,384]{1,0:T(8,128)(2,1)} %single_h.1, s32[1,128]{1,0:T(1,128)} %bitcast.9, s32[1,128]{1,0:T(1,128)} %bitcast.10, s32[1,128]{1,0:T(1,128)} %bitcast.11, s32[1,128]{1,0:T(1,128)} %bitcast.12, ...), custom_call_target="tpu_custom_call" | custom-call | tf_op jit(solution)/shard_map/confidence/pallas_call | solution.py:471
  17.5 0.6 %place.1 = (bf16[8,384]{1,0:T(8,128)(2,1)}, f32[8,128]{1,0:T(8,128)}) custom-call(bf16[8,384]{1,0:T(8,128)(2,1)S(1)} %get-tuple-element.4.refined_v, f32[8,128]{1,0:T(8,128)S(1)} %get-tuple-element.5.errors_v), custom_call_target="tpu_custom_call" | custom-call | tf_op jit(solution)/shard_map/place/pallas_call | solution.py:481

commit v7 on v6

--- a/solution.py
+++ b/solution.py
@@ -57,6 +57,7 @@
     wq_v, wk_v, wv_v, wg_v, wo_v, wb_v, rel_v, wma_v, wmb_v, wha_v, whb_v, who_v, wp_v, pb_v,
     code_v, ccol_v, mask_v, bias_s, bias_r, norm_s, norm_r, pair_r, b_s, b_r, a_v, pin_v,
     flat_v, x_v, hid_v, wab_v, scale_v, square_v, score_v,
+    two_v, gate_v, toward_v, sum_v, a_s, a_r, refined_s, refined_r,
     local_sem, send_sem, recv_sem,
 ):
     me = lax.axis_index("rows")
@@ -124,7 +125,8 @@
     center = jnp.mean(mine, axis=-1, keepdims=True)
     normed = norm_rows(mine).astype(bf16)
     norm_s[...] = normed
-    norm_r[me // 2, me % 2] = normed
+    norm_r[me] = normed
+    two_v[me % 2] = single_v[...]
 
     arrive(REL, WB, PAIR)
     rel = rel_v[...]
@@ -150,26 +152,23 @@
         return 0
 
     lax.fori_loop(0, count // step, bias_block, 0, unroll=short)
-    bias_r[me] = bias_s[me]
+    bias_r[me] = bias_s[pl.ds(me - me % 2, 2)]
 
     pl.semaphore_wait(barrier, n - 1)
 
-    def remote(src, dst, i, k, peer):
+    def remote(src, dst, i, at, peer):
         pltpu.make_async_remote_copy(
-            src_ref=src, dst_ref=dst, send_sem=send_sem.at[i], recv_sem=recv_sem.at[i, k],
+            src_ref=src, dst_ref=dst, send_sem=send_sem.at[i], recv_sem=recv_sem.at[at],
             device_id={"rows": peer}, device_id_type=pl.DeviceIdType.MESH).start()
 
     side = me % 2
+    chip = me - side
     partner = me + 1 - 2 * side
     pairs = size // 2
 
-    def spread_single(k):
-        base = groups[k] * size
-
+    def each_chip(k, visit):
         def body(s, _):
-            chip = base + 2 * ((mine_at // 2 + s) % pairs)
-            for core in (0, 1) if k == 0 else (side,):
-                remote(norm_s, norm_r.at[me // 2, side], 0, k, chip + core)
+            visit(groups[k] * size + 2 * ((mine_at // 2 + s) % pairs))
             return 0
 
         if short:
@@ -177,17 +176,24 @@
                 body(s, 0)
         else:
             lax.fori_loop(1 if k == 0 else 0, pairs, body, 0)
-        if k == 0:
-            remote(norm_s, norm_r.at[me // 2, side], 5, 0, partner)
+
+    @pl.when(side == 0)
+    def _():
+        remote(norm_s, norm_r.at[me], 4, (4, 0), partner)
+        remote(single_v, two_v.at[0], 5, (4, 1), partner)
 
     for k in reversed(range(parts)):
-        spread_single(k)
+        each_chip(k, lambda to: remote(norm_s, norm_r.at[me], 0, (0, k), to + 1))
     for k in reversed(range(parts)):
-        each_peer(k, lambda peer: remote(bias_s.at[peer], bias_r.at[me], 1, k, peer))
+        each_chip(k, lambda to: remote(bias_s.at[pl.ds(to, 2)], bias_r.at[me], 1, (1, k), to + 1))
+
+    @pl.when(side == 0)
+    def _():
+        remote(bias_s.at[pl.ds(chip, 2)], bias_r.at[me], 6, (4, 2), partner)
 
     def send_pair(k):
         each_peer(k, lambda peer: remote(
-            pair_v.at[pl.ds(peer * rows, rows)], pair_r.at[me], 2, k, peer))
+            pair_v.at[pl.ds(peer * rows, rows)], pair_r.at[me], 2, (2, k), peer))
 
     def send_pair_either(edge, middle, low, high):
         inside = group * (3 - group) // 2
@@ -196,7 +202,7 @@
 
         def body(s, _):
             peer = base + (mine_at + s) % size
-            remote(pair_v.at[pl.ds(peer * rows, rows)], pair_r.at[me], 2, k, peer)
+            remote(pair_v.at[pl.ds(peer * rows, rows)], pair_r.at[me], 2, (2, k), peer)
             return 0
 
         if short:
@@ -205,30 +211,38 @@
         else:
             lax.fori_loop(low, high, body, 0)
 
-    arrive(WQ)
-    queries = mm(normed, wq_v[...]).astype(bf16).astype(f32)
-    arrive(WG)
-    gating = jax.nn.sigmoid(mm(normed, wg_v[...]))
+    def landed(buf, at):
+        pltpu.make_async_copy(buf, buf, recv_sem.at[at]).wait()
+
+    arrive(COMPLEX, PAD, WQ, WG, WK)
     head_of = lax.broadcasted_iota(jnp.int32, (rows, inner), 1) // head_size
-    q_wide = jnp.concatenate(
-        [jnp.where(head_of == h, queries, 0.0) for h in range(heads)], axis=0).astype(bf16)
-    arrive(WK)
-    toward = (mm_nt(wk_v[...], q_wide) / math.sqrt(head_size)).astype(bf16)
-
-    arrive(COMPLEX, PAD)
-    lane_spot = lax.broadcasted_iota(jnp.int32, (step, spots), 1) % rows
-    for k in range(0, count, step):
-        ccol_v[k:k + step, :] = jnp.broadcast_to(
-            column(complex_v[:, k:k + step].astype(f32)), (step, 128))
-    mine_c = ccol_v[pl.ds(first, rows), 0:1]
-    lane_row = lax.broadcasted_iota(jnp.int32, (rows, spots), 1) % rows
-    pick = lane_row == lax.broadcasted_iota(jnp.int32, (rows, spots), 0)
-    query_c = jnp.sum(jnp.where(pick, mine_c, 0.0), axis=0, keepdims=True)
-    for k in range(0, count, step):
-        real = column(pad_v[:, k:k + step].astype(f32)) == 1.0
-        same = ccol_v[k:k + step, :spots] == query_c
-        itself = (lax.broadcasted_iota(jnp.int32, (step, spots), 0) + k) == (first + lane_spot)
-        mask_v[k:k + step, :] = jnp.where(same & (real | itself), 0.0, masked_score)
+
+    @pl.when(side == 1)
+    def _():
+        landed(norm_s, (4, 0))
+        both = norm_r[pl.ds(chip, 2)].astype(f32).reshape(2 * rows, inner).astype(bf16)
+        queries = mm(both, wq_v[...]).astype(bf16).astype(f32)
+        gate_v[...] = jax.nn.sigmoid(mm(both, wg_v[...]))
+        q_wide = jnp.concatenate(
+            [jnp.where(head_of == h, queries[c * rows:(c + 1) * rows], 0.0)
+             for c in (0, 1) for h in range(heads)], axis=0).astype(bf16)
+        toward_v[...] = (mm_nt(wk_v[...], q_wide) / math.sqrt(head_size)).astype(bf16)
+        lane_spot = lax.broadcasted_iota(jnp.int32, (step, spots), 1) % rows
+        for k in range(0, count, step):
+            ccol_v[k:k + step, :] = jnp.broadcast_to(
+                column(complex_v[:, k:k + step].astype(f32)), (step, 128))
+        lane_row = lax.broadcasted_iota(jnp.int32, (rows, spots), 1) % rows
+        pick = lane_row == lax.broadcasted_iota(jnp.int32, (rows, spots), 0)
+        for c in (0, 1):
+            start = (chip + c) * rows
+            mine_c = ccol_v[pl.ds(pl.multiple_of(start, rows), rows), 0:1]
+            query_c = jnp.sum(jnp.where(pick, mine_c, 0.0), axis=0, keepdims=True)
+            for k in range(0, count, step):
+                real = column(pad_v[:, k:k + step].astype(f32)) == 1.0
+                same = ccol_v[k:k + step, :spots] == query_c
+                itself = (lax.broadcasted_iota(jnp.int32, (step, spots), 0) + k) == (start + lane_spot)
+                mask_v[k:k + step, c * spots:(c + 1) * spots] = jnp.where(
+                    same & (real | itself), 0.0, masked_score)
 
     def rel_block(q, _):
         diff = code_v[pl.ds(first + q, 1), :classes] - code_v[:, :classes]
@@ -248,59 +262,69 @@
     arrive(WV, WO, WMB, WMA)
     wab_v[:, :width] = wmb_v[...]
     wab_v[:, width:] = wma_v[...]
-    wab_sum = mm(jnp.ones((rows, inner), bf16), wab_v[...])
+    sum_v[...] = mm(jnp.ones((rows, inner), bf16), wab_v[...])
 
     pair_r[me] = pair_v[pl.ds(first, rows)]
-
-    def take_single(k):
-        if k == 0:
-            if pairs > 1:
-                landed = norm_r.at[pl.ds(0, pairs - 1)]
-                pltpu.make_async_copy(landed, landed, recv_sem.at[0, 0]).wait()
-            pltpu.make_async_copy(norm_s, norm_s, recv_sem.at[5, 0]).wait()
-        else:
-            half = norm_r.at[pl.ds(groups[k] * pairs, pairs), side]
-            pltpu.make_async_copy(half, half, recv_sem.at[0, k]).wait()
-            remote(half, half, 4, k, partner)
 
     send_pair_either(3, 2, 0, size)
     send_pair(1)
     send_pair(0)
     send_pair_either(2, 3, 0, size * 2 // 4)
-    for k in range(parts):
-        take_single(k)
-    for k in range(1, parts):
-        half = norm_r.at[pl.ds(0, pairs), 0]
-        pltpu.make_async_copy(half, half, recv_sem.at[4, k]).wait()
-    every = norm_r[...].astype(f32).reshape(count, inner).astype(bf16)
-    score_v[...] = mm(every, toward) + mask_v[...]
-    for k in range(parts):
-        take(bias_r, recv_sem.at[1], k)
-    values = mm(every, wv_v[...]).astype(bf16)
-    scores = score_v[...] + bias_r[...].astype(f32).reshape(count, spots)
-    expo = jnp.exp(scores - jnp.max(scores, axis=0, keepdims=True))
-    weights = (expo * (1.0 / jnp.sum(expo, axis=0, keepdims=True))).astype(bf16)
-    mixed_heads = mm_tn(weights, values)
-    attended = mixed_heads[:rows, :]
-    for h in range(1, heads):
-        attended = jnp.where(head_of == h, mixed_heads[h * rows:(h + 1) * rows, :], attended)
-    refined = (mine + mm((gating * attended).astype(bf16), wo_v[...])).astype(bf16)
-    raw = mm(refined, wab_v[...])
-    exact = refined.astype(f32)
-    away = exact - center
-    shift = jnp.mean(away, axis=-1, keepdims=True)
-    spread = jnp.maximum(jnp.mean(away * away, axis=-1, keepdims=True) - shift * shift, 0.0)
-    middle = center + shift
-    scale = lax.rsqrt(spread + epsilon)
-    factors = ((raw - middle * wab_sum) * scale).astype(bf16)
-    factor_b = factors[:, :width]
-    b_s[...] = factor_b
-    a_v[...] = factors[:, width:].astype(f32)
-    b_r[me] = factor_b
-    refined_ref[...] = refined
-
-    for k in reversed(range(parts)):
-        each_peer(k, lambda peer: remote(b_s, b_r.at[me], 3, k, peer))
+
+    @pl.when(side == 1)
+    def _():
+        for k in range(parts):
+            landed(norm_r.at[pl.ds(0, size - (2 if k == 0 else 0))], (0, k))
+        every = norm_r[...].astype(f32).reshape(count, inner).astype(bf16)
+        score_v[...] = mm(every, toward_v[...]) + mask_v[...]
+        landed(two_v.at[0], (4, 1))
+        landed(bias_s.at[pl.ds(0, 2)], (4, 2))
+        for k in range(parts):
+            landed(bias_r.at[pl.ds(0, size - (2 if k == 0 else 0))], (1, k))
+        values = mm(every, wv_v[...]).astype(bf16)
+        attended = []
+        for c in (0, 1):
+            scores = (score_v[:, c * spots:(c + 1) * spots]
+                      + bias_r[:, c].astype(f32).reshape(count, spots))
+            expo = jnp.exp(scores - jnp.max(scores, axis=0, keepdims=True))
+            weights = (expo * (1.0 / jnp.sum(expo, axis=0, keepdims=True))).astype(bf16)
+            mixed_heads = mm_tn(weights, values)
+            found = mixed_heads[:rows, :]
+            for h in range(1, heads):
+                found = jnp.where(head_of == h, mixed_heads[h * rows:(h + 1) * rows, :], found)
+            attended.append(found)
+        attended = jnp.concatenate(attended, axis=0)
+        before = two_v[...].astype(f32).reshape(2 * rows, inner)
+        center = jnp.mean(before, axis=-1, keepdims=True)
+        refined = (before + mm((gate_v[...] * attended).astype(bf16), wo_v[...])).astype(bf16)
+        raw = mm(refined, wab_v[...])
+        away = refined.astype(f32) - center
+        shift = jnp.mean(away, axis=-1, keepdims=True)
+        spread = jnp.maximum(jnp.mean(away * away, axis=-1, keepdims=True) - shift * shift, 0.0)
+        factors = ((raw - (center + shift) * sum_v[0:1, :]) * lax.rsqrt(spread + epsilon))
+        factors = factors.astype(bf16).astype(f32)
+        for c in (0, 1):
+            b_s[c] = factors[c * rows:(c + 1) * rows, :width].astype(bf16)
+            b_r[chip + c] = factors[c * rows:(c + 1) * rows, :width].astype(bf16)
+        a_s[...] = factors[:rows, width:].astype(bf16)
+        refined_s[...] = refined.astype(f32)[:rows].astype(bf16)
+        for k in reversed(range(parts)):
+            each_chip(k, lambda to: remote(b_s, b_r.at[pl.ds(chip, 2)], 7, (3, k), to))
+            each_chip(k, lambda to: remote(b_s, b_r.at[pl.ds(chip, 2)], 3, (3, k), to + 1))
+        remote(b_s, b_r.at[pl.ds(chip, 2)], 8, (5, 0), partner)
+        remote(a_s, a_r, 9, (5, 1), partner)
+        remote(refined_s, refined_r, 10, (5, 2), partner)
+        a_v[...] = factors[rows:, width:]
+        refined_ref[...] = refined.astype(f32)[rows:].astype(bf16)
+
+    @pl.when(side == 0)
+    def _():
+        landed(b_s, (5, 0))
+        landed(a_s, (5, 1))
+        landed(refined_s, (5, 2))
+        a_v[...] = a_r[...].astype(f32)
+        refined_ref[...] = refined_r[...]
+
     send_pair_either(2, 3, size * 2 // 4, size)
 
     per = step // sub
@@ -366,26 +390,26 @@
 
     def ready(k):
         take(pair_r, recv_sem.at[2], k)
-        take(b_r, recv_sem.at[3], k)
+        landed(b_r.at[pl.ds(0, size - (2 if k == 0 else 0))], (3, k))
 
     errors_ref[...] = jnp.zeros_like(errors_ref)
     if short and parts == 4:
-        take(b_r, recv_sem.at[3], 0)
+        landed(b_r.at[pl.ds(0, size - 2)], (3, 0))
         take(pair_r, recv_sem.at[2], 0)
-        take(b_r, recv_sem.at[3], 1)
+        landed(b_r.at[pl.ds(0, size)], (3, 1))
         take(pair_r, recv_sem.at[2], 1)
         mix(0, 0)
         mix(1, 0)
         expand((0,1,))
         reduce(0)
         reduce(1)
-        take(b_r, recv_sem.at[3], 2)
+        landed(b_r.at[pl.ds(0, size)], (3, 2))
         take(pair_r, recv_sem.at[2], 2)
         mix(2, 0)
         grade(0, 0)
         grade(1, 0)
         expand((2,))
-        take(b_r, recv_sem.at[3], 3)
+        landed(b_r.at[pl.ds(0, size)], (3, 3))
         take(pair_r, recv_sem.at[2], 3)
         mix(3, 0)
         reduce(2)
@@ -411,14 +435,23 @@
         out = buf.at[pl.ds(0, amount)]
         pltpu.make_async_copy(out, out, send_sem.at[i]).wait()
 
-    sent(bias_r, 1, n - 1)
+    sent(norm_r, 0, n // 2 - 1)
+    sent(bias_r, 1, n // 2 - 1)
     sent(pair_r, 2, n - 1)
-    sent(b_r, 3, n - 1)
-    pltpu.make_async_copy(norm_s, norm_s, send_sem.at[5]).wait()
-    if n > 2:
-        sent(norm_r, 0, (size - 2 + (parts - 1) * pairs) // 2)
-    if parts > 1:
-        sent(norm_r, 4, (parts - 1) * pairs // 2)
+
+    @pl.when(side == 0)
+    def _():
+        pltpu.make_async_copy(norm_s, norm_s, send_sem.at[4]).wait()
+        pltpu.make_async_copy(single_v, single_v, send_sem.at[5]).wait()
+        sent(bias_s, 6, 2)
+
+    @pl.when(side == 1)
+    def _():
+        sent(b_r, 3, n - 2)
+        sent(b_r, 7, n - 2)
+        pltpu.make_async_copy(b_s, b_s, send_sem.at[8]).wait()
+        pltpu.make_async_copy(a_s, a_s, send_sem.at[9]).wait()
+        pltpu.make_async_copy(refined_s, refined_s, send_sem.at[10]).wait()
 
 
 def place(refined_v, errors_v, refined_h, errors_h, sem):
@@ -447,13 +480,13 @@
     scratch = [pltpu.VMEM(a.shape, a.dtype) for a in args] + [
         pltpu.VMEM((count, 128), f32),
         pltpu.VMEM((count, 128), f32),
-        pltpu.VMEM((count, spots), f32),
+        pltpu.VMEM((count, 2 * spots), f32),
         pltpu.VMEM((n, rows, spots), bf16),
-        pltpu.VMEM((n, rows, spots), bf16),
+        pltpu.VMEM((n, 2, rows, spots), bf16),
         pltpu.VMEM((rows, inner), bf16),
-        pltpu.VMEM((n // 2, 2, rows, inner), bf16),
+        pltpu.VMEM((n, rows, inner), bf16),
         pltpu.VMEM((n, rows, rows, width), bf16),
-        pltpu.VMEM((rows, width), bf16),
+        pltpu.VMEM((2, rows, width), bf16),
         pltpu.VMEM((n, rows, width), bf16),
         pltpu.VMEM((rows, width), f32),
         pltpu.VMEM((rows, count, width), f32),
@@ -463,9 +496,17 @@
         pltpu.VMEM((inner, 2 * width), bf16),
         pltpu.VMEM((rows * step, 128), f32),
         pltpu.VMEM((rows * step, width), bf16),
-        pltpu.VMEM((count, spots), f32),
+        pltpu.VMEM((count, 2 * spots), f32),
+        pltpu.VMEM((2, rows, inner), bf16),
+        pltpu.VMEM((2 * rows, inner), f32),
+        pltpu.VMEM((inner, 2 * spots), bf16),
+        pltpu.VMEM((rows, 2 * width), f32),
+        pltpu.VMEM((rows, width), bf16),
+        pltpu.VMEM((rows, width), bf16),
+        pltpu.VMEM((rows, inner), bf16),
+        pltpu.VMEM((rows, inner), bf16),
         pltpu.SemaphoreType.DMA((len(args),)),
-        pltpu.SemaphoreType.DMA((6,)),
+        pltpu.SemaphoreType.DMA((11,)),
         pltpu.SemaphoreType.DMA((6, 4)),
     ]
     refined, errors = pl.pallas_call(

time: 18.3 us -> 17.8 us (0.973)
  Pallas kernels: 17.5 us -> 17 us
    pallas_call x1, Pallas kernels: 16.9 us -> 16.4 us  [on_device(): pl.pallas_call(functools.partial(kernel, n, heads), out_shape=(pltpu.VMEM...]
where the time goes in v7:
time: 17.8 us; the launch traced here: 17.6 us
  Pallas kernels  17 us (96%)
  between operations  0.65 us (4%)
    pallas_call x1, Pallas kernels, on_device(): pl.pallas_call(functools.partial(kernel, n, heads), out_shape=(pltpu.VMEM...  16.4 us
    pallas_call x1, Pallas kernels, on_device(): pl.pallas_call(place, out_shape=(jax.ShapeDtypeStruct((rows, inner), bf16...  0.62 us

profile of v7, /device:TPU:0, one launch (start us, length us, event | category | flops | bytes accessed | tf_op | source)
XLA Modules:
  0.0 17.6 jit_solution(3177115716007807003)
XLA Ops:
  0.6 16.4 %confidence.1 = (bf16[8,384]{1,0:T(8,128)(2,1)S(1)}, f32[8,128]{1,0:T(8,128)S(1)}) custom-call(bf16[128,8,128]{2,1,0:T(8,128)(2,1)} %pair_h.1, bf16[8,384]{1,0:T(8,128)(2,1)} %single_h.1, s32[1,128]{1,0:T(1,128)} %bitcast.9, s32[1,128]{1,0:T(1,128)} %bitcast.10, s32[1,128]{1,0:T(1,128)} %bitcast.11, s32[1,128]{1,0:T(1,128)} %bitcast.12, ...), custom_call_target="tpu_custom_call" | custom-call | tf_op jit(solution)/shard_map/confidence/pallas_call | solution.py:512
  17.0 0.6 %place.1 = (bf16[8,384]{1,0:T(8,128)(2,1)}, f32[8,128]{1,0:T(8,128)}) custom-call(bf16[8,384]{1,0:T(8,128)(2,1)S(1)} %get-tuple-element.4.refined_v, f32[8,128]{1,0:T(8,128)S(1)} %get-tuple-element.5.errors_v), custom_call_target="tpu_custom_call" | custom-call | tf_op jit(solution)/shard_map/place/pallas_call | solution.py:522

commit v8 on v7

--- a/solution.py
+++ b/solution.py
@@ -269,7 +269,7 @@
     send_pair_either(3, 2, 0, size)
     send_pair(1)
     send_pair(0)
-    send_pair_either(2, 3, 0, size * 2 // 4)
+    send_pair_either(2, 3, 0, size * 1 // 4)
 
     @pl.when(side == 1)
     def _():
@@ -325,7 +325,7 @@
         a_v[...] = a_r[...].astype(f32)
         refined_ref[...] = refined_r[...]
 
-    send_pair_either(2, 3, size * 2 // 4, size)
+    send_pair_either(2, 3, size * 1 // 4, size)
 
     per = step // sub
     lane_part = lax.broadcasted_iota(jnp.int32, (rows, step), 1) // sub
@@ -400,22 +400,23 @@
         take(pair_r, recv_sem.at[2], 1)
         mix(0, 0)
         mix(1, 0)
-        expand((0,1,))
+        expand((0,))
+        expand((1,))
         reduce(0)
         reduce(1)
         landed(b_r.at[pl.ds(0, size)], (3, 2))
         take(pair_r, recv_sem.at[2], 2)
+        landed(b_r.at[pl.ds(0, size)], (3, 3))
+        take(pair_r, recv_sem.at[2], 3)
         mix(2, 0)
         grade(0, 0)
+        mix(3, 0)
+        expand((2,))
         grade(1, 0)
-        expand((2,))
-        landed(b_r.at[pl.ds(0, size)], (3, 3))
-        take(pair_r, recv_sem.at[2], 3)
-        mix(3, 0)
+        expand((3,))
         reduce(2)
-        expand((3,))
+        reduce(3)
         grade(2, 0)
-        reduce(3)
         grade(3, 0)
     else:
         for k in range(parts):

time: 17.8 us -> 17.5 us (0.983)
  Pallas kernels: 17 us -> 16.7 us
    pallas_call x1, Pallas kernels: 16.4 us -> 16 us  [on_device(): pl.pallas_call(functools.partial(kernel, n, heads), out_shape=(pltpu.VMEM...]
where the time goes in v8:
time: 17.5 us; the launch traced here: 17.3 us
  Pallas kernels  16.7 us (95%)
  between operations  0.65 us (4%)
    pallas_call x1, Pallas kernels, on_device(): pl.pallas_call(functools.partial(kernel, n, heads), out_shape=(pltpu.VMEM...  16 us
    pallas_call x1, Pallas kernels, on_device(): pl.pallas_call(place, out_shape=(jax.ShapeDtypeStruct((rows, inner), bf16...  0.62 us

profile of v8, /device:TPU:0, one launch (start us, length us, event | category | flops | bytes accessed | tf_op | source)
XLA Modules:
  0.0 17.3 jit_solution(17272604501769032766)
XLA Ops:
  0.6 16.0 %confidence.1 = (bf16[8,384]{1,0:T(8,128)(2,1)S(1)}, f32[8,128]{1,0:T(8,128)S(1)}) custom-call(bf16[128,8,128]{2,1,0:T(8,128)(2,1)} %pair_h.1, bf16[8,384]{1,0:T(8,128)(2,1)} %single_h.1, s32[1,128]{1,0:T(1,128)} %bitcast.9, s32[1,128]{1,0:T(1,128)} %bitcast.10, s32[1,128]{1,0:T(1,128)} %bitcast.11, s32[1,128]{1,0:T(1,128)} %bitcast.12, ...), custom_call_target="tpu_custom_call" | custom-call | tf_op jit(solution)/shard_map/confidence/pallas_call | solution.py:513
  16.7 0.6 %place.1 = (bf16[8,384]{1,0:T(8,128)(2,1)}, f32[8,128]{1,0:T(8,128)}) custom-call(bf16[8,384]{1,0:T(8,128)(2,1)S(1)} %get-tuple-element.4.refined_v, f32[8,128]{1,0:T(8,128)S(1)} %get-tuple-element.5.errors_v), custom_call_target="tpu_custom_call" | custom-call | tf_op jit(solution)/shard_map/place/pallas_call | solution.py:523
